TPU v7x, 8 devices: a whole 2x2x1 slice. The times are simulated.
8 devices in a mesh: dom: 2 (over z, y), ens: 4 (over x, core).
Axes of the slice: x: 2, y: 2, z: 1, core: 2. Of those that a mesh axis runs over, the one named last changes fastest.
Arguments:
- ens_state: bfloat16 [64, 128, 32, 227], P('ens', None, 'dom')
- w_in: bfloat16 [454, 512], replicated
- w_out: bfloat16 [512, 227], replicated
- obs_op: bfloat16 [227, 32], replicated
- obs_val: float32 [32, 4, 2, 16, 32], P(None, None, 'dom')
- obs_wt: float32 [32, 4, 2, 16, 32], P(None, None, 'dom')
Outputs:
- output: bfloat16 [128, 32, 64, 227], P('ens', 'dom')
All inputs are finite; a program needn't handle non-finite values.
Results may differ from a plain program's by a relative error of at most 0.001.
Values are sent between devices in bfloat16 or wider.
A program may use at most 1 GiB of HBM per device.

v0:
```python
import math
import jax
import jax.numpy as jnp
from jax import lax
from jax.sharding import PartitionSpec as P, NamedSharding

NS_STEPS = 18
FULL_PRECISION = lax.Precision.HIGHEST


def five_point(ens_state, west_ghost, east_ghost):
    west_val = jnp.concatenate([west_ghost, ens_state[:, :, :-1]], axis=2).astype(jnp.float32)
    east_val = jnp.concatenate([ens_state[:, :, 1:], east_ghost], axis=2).astype(jnp.float32)
    north_val = jnp.concatenate([ens_state[:, :1], ens_state[:, :-1]], axis=1).astype(jnp.float32)
    south_val = jnp.concatenate([ens_state[:, 1:], ens_state[:, -1:]], axis=1).astype(jnp.float32)
    total = north_val + south_val + west_val + east_val - 4.0 * ens_state.astype(jnp.float32)
    return total.astype(jnp.bfloat16)


def value_a13(ens_state, lap_field, w_in, w_out, row_start, rows_dev):
    channels = ens_state.shape[-1]
    state_blk = lax.dynamic_slice_in_dim(ens_state, row_start, rows_dev, axis=1)
    lap_blk = lax.dynamic_slice_in_dim(lap_field, row_start, rows_dev, axis=1)
    hidden = jnp.einsum("mijc,cf->mijf", state_blk, w_in[:channels], preferred_element_type=jnp.float32)
    hidden = hidden + jnp.einsum("mijc,cf->mijf", lap_blk, w_in[channels:], preferred_element_type=jnp.float32)
    gelu_out = jax.nn.gelu(hidden, approximate=True).astype(jnp.bfloat16)
    increment = jnp.einsum("mijf,fc->mijc", gelu_out, w_out, preferred_element_type=jnp.float32)
    return (state_blk.astype(jnp.float32) + increment).astype(jnp.bfloat16)


def patch_analysis(value_a8, obs_op, obs_val, obs_wt):
    members, rows, columns, channels = value_a8.shape
    patch_rows, tile_height, patch_cols, tile_width = obs_val.shape[:4]
    fc_tiles = value_a8.reshape(members, patch_rows, tile_height, patch_cols, tile_width, channels)
    mean_fc = jnp.mean(fc_tiles, axis=0, dtype=jnp.float32)
    anomaly = fc_tiles.astype(jnp.float32) - mean_fc
    obs_fc = jnp.einsum("kprqsc,co->kprqso", fc_tiles, obs_op, preferred_element_type=jnp.float32)
    obs_mean = jnp.mean(obs_fc, axis=0)
    obs_anom = obs_fc - obs_mean
    weighted = obs_anom * obs_wt
    identity = jnp.eye(members, dtype=jnp.float32)
    a_mat = (members - 1.0) * identity + jnp.einsum("kprqso,lprqso->pqkl", weighted, obs_anom, precision=FULL_PRECISION)
    obs_proj = jnp.einsum("kprqso,prqso->pqk", weighted, obs_val - obs_mean, precision=FULL_PRECISION)
    a_trace = jnp.trace(a_mat, axis1=2, axis2=3)[:, :, None, None]

    def newton_step(step_idx, carry):
        sqrt_est, inv_est = carry
        mixer = 1.5 * identity - 0.5 * jnp.einsum("pqij,pqjk->pqik", inv_est, sqrt_est, precision=FULL_PRECISION)
        return (jnp.einsum("pqij,pqjk->pqik", sqrt_est, mixer, precision=FULL_PRECISION), jnp.einsum("pqij,pqjk->pqik", mixer, inv_est, precision=FULL_PRECISION))

    start_pair = (a_mat / a_trace, jnp.broadcast_to(identity, a_mat.shape))
    sqrt_est, inv_est = lax.fori_loop(0, NS_STEPS, newton_step, start_pair)
    inv_root = inv_est / jnp.sqrt(a_trace)
    post_cov = jnp.einsum("pqij,pqjk->pqik", inv_root, inv_root, precision=FULL_PRECISION)
    w_mean = jnp.einsum("pqkl,pql->pqk", post_cov, obs_proj, precision=FULL_PRECISION)
    transform = math.sqrt(members - 1.0) * inv_root + w_mean[:, :, :, None]
    update = jnp.einsum("kprqsc,pqke->prqsec", anomaly, transform, precision=FULL_PRECISION)
    analysis = (mean_fc[:, :, :, :, None, :] + update).astype(jnp.bfloat16)
    return analysis.reshape(rows, columns, members, channels)


def solution(mesh):
    dom_size = mesh.shape["dom"]
    ens_size = mesh.shape["ens"]
    to_east = [(source, (source + 1) % dom_size) for source in range(dom_size)]
    to_west = [(source, (source - 1) % dom_size) for source in range(dom_size)]
    obs_spec = P(None, None, "dom", None, None)

    def local_step(ens_state, w_in, w_out, obs_op, obs_val, obs_wt):
        local_members, rows, columns, channels = ens_state.shape
        rows_dev = rows // ens_size
        west_ghost = lax.ppermute(ens_state[:, :, -1:], "dom", to_east)
        east_ghost = lax.ppermute(ens_state[:, :, :1], "dom", to_west)
        lap_field = five_point(ens_state, west_ghost, east_ghost)

        def value_a14(block_idx):
            return value_a13(ens_state, lap_field, w_in, w_out, block_idx * rows_dev, rows_dev)

        fc_blocks = lax.map(value_a14, jnp.arange(ens_size))
        received = lax.all_to_all(fc_blocks, "ens", 0, 0, tiled=True)
        value_a8 = received.reshape(ens_size * local_members, rows_dev, columns, channels)
        tile_rows = obs_val.shape[0] // ens_size
        row_start = lax.axis_index("ens") * tile_rows
        obs_local = lax.dynamic_slice_in_dim(obs_val, row_start, tile_rows, axis=0)
        wt_local = lax.dynamic_slice_in_dim(obs_wt, row_start, tile_rows, axis=0)
        return patch_analysis(value_a8, obs_op, obs_local, wt_local)

    return jax.shard_map(local_step, mesh=mesh, in_specs=(P("ens", None, "dom", None), P(), P(), P(), obs_spec, obs_spec), out_specs=P("ens", "dom", None, None), check_vma=False)
```

profile of v0, /device:TPU:1, one launch (start us, length us, event | category | flops | bytes accessed | tf_op | source)
XLA Modules:
  0.0 623.2 jit_solution(9770128587770238704)
XLA Ops:
  0.0 8.2 %fusion.65 = (bf16[16,128,1,227]{1,2,3,0:T(2,128)(2,1)S(1)}, bf16[16,128,1,227]{1,2,3,0:T(2,128)(2,1)S(1)}) fusion(bf16[16,128,16,227]{1,2,3,0:T(8,128)(2,1)} %param.10), kind=kLoop, calls=%fused_computation.74 | loop fusion | bytes 3719168 | tf_op jit(solution)/shard_map/slice | solution.py:73
  8.2 1.1 copy.60
  9.3 2.1 collective-permute-start
  11.4 1.1 copy.61
  12.5 24.9 %copy.39 = bf16[16,128,16,227]{3,2,1,0:T(8,128)(2,1)} copy(bf16[16,128,16,227]{1,2,3,0:T(8,128)(2,1)} %param.10) | data formatting | bytes 29753344 | tf_op jit(solution)/shard_map/while | solution.py:79
  37.4 26.4 %fusion.62 = (bf16[16,128,15,227]{3,2,1,0:T(8,128)(2,1)}, bf16[16,128,15,227]{3,2,1,0:T(8,128)(2,1)}) fusion(bf16[16,128,16,227]{3,2,1,0:T(8,128)(2,1)} %copy.39), kind=kLoop, calls=%fused_computation.71 | loop fusion | bytes 55787520 | tf_op jit(solution)/shard_map/slice | solution.py:13
  63.8 11.2 %fusion.63 = (bf16[16,127,16,227]{3,2,1,0:T(8,128)(2,1)}, bf16[16,127,16,227]{3,2,1,0:T(8,128)(2,1)}) fusion(bf16[16,128,16,227]{3,2,1,0:T(8,128)(2,1)S(1)} %copy-done.1), kind=kLoop, calls=%fused_computation.72 | loop fusion | bytes 59041792 | tf_op jit(solution)/shard_map/slice | solution.py:15
  75.0 1.0 fusion.64
  76.0 3.8 copy.34
  79.9 4.5 copy.37
  84.4 38.6 %subtract_convert_fusion = bf16[16,128,16,227]{3,2,1,0:T(8,128)(2,1)} fusion(bf16[16,128,16,227]{3,2,1,0:T(8,128)(2,1)} %copy.39, bf16[16,127,16,227]{3,2,1,0:T(8,128)(2,1)} %get-tuple-element.119, bf16[16,1,16,227]{3,2,1,0:T(8,128)(2,1)S(1)} %get-tuple-element.121, bf16[16,1,16,227]{3,2,1,0:T(8,128)(2,1)S(1)} %get-tuple-element.120, ...), kind=kLoop, calls=%fused_computation.43 | loop fusion | flops 171081728 | bytes 89260032 | tf_op jit(solution)/shard_map/convert_element_type | solution.py:17
  122.9 99.4 %while.23 = (s32[]{:T(128)}, bf16[4,16,32,16,227]{4,3,2,1,0:T(8,128)(2,1)}, s32[4]{0:T(128)S(1)}, bf16[16,128,16,227]{3,2,1,0:T(8,128)(2,1)}, bf16[454,512]{1,0:...) while((s32[]{:T(128)}, ...), condition=%wide.region_1.2_spmd, body=%wide.region_0.1_spmd.sunk | while | flops 5760163840 | bytes 53835488 | solution.py:79
  123.1 0.6 dynamic_slice.34
  124.4 10.3 %fusion.96 = f32[16,32,16,512]{3,2,1,0:T(8,128)} fusion(bf16[16,128,16,227]{3,2,1,0:T(8,128)(2,1)} %get-tuple-element.215, s32[]{:T(128)S(6)} %select_n.18, bf16[454,512]{1,0:T(8,128)(2,1)} %get-tuple-element.216), kind=kOutput, calls=%fused_computation.14.clone.1 | convolution fusion | flops 1904214016 | bytes 21209092 | tf_op jit(solution)/shard_map/while/body/eval_jaxpr/mijc,cf->mijf/dot_general | solution.py:24
  134.6 13.3 %fusion.97 = bf16[4,16,32,16,227]{4,3,2,1,0:T(8,128)(2,1)} fusion(bf16[4,16,32,16,227]{4,3,2,1,0:T(8,128)(2,1)} %get-tuple-element.202, s32[]{:T(128)} %get-tuple-element.201, bf16[16,128,16,227]{3,2,1,0:T(8,128)(2,1)} %get-tuple-element.215, s32[]{:T(128)S(6)} %select_n.18, f32[16,32,16,512]{3,2,1,0:T(8,128)} %fusion.96, ...), kind=kOutput, calls=%fused_computation.12.clone.1 | convolution fusion | flops 3855949824 | bytes 29836800 | tf_op jit(solution)/shard_map/while/body/eval_jaxpr/mijf,fc->mijc/dot_general | solution.py:27
  147.9 0.6 dynamic_slice.34
  149.2 10.3 %fusion.96 = f32[16,32,16,512]{3,2,1,0:T(8,128)} fusion(bf16[16,128,16,227]{3,2,1,0:T(8,128)(2,1)} %get-tuple-element.215, s32[]{:T(128)S(6)} %select_n.18, bf16[454,512]{1,0:T(8,128)(2,1)} %get-tuple-element.216), kind=kOutput, calls=%fused_computation.14.clone.1 | convolution fusion | flops 1904214016 | bytes 21209092 | tf_op jit(solution)/shard_map/while/body/eval_jaxpr/mijc,cf->mijf/dot_general | solution.py:24
  159.4 13.3 %fusion.97 = bf16[4,16,32,16,227]{4,3,2,1,0:T(8,128)(2,1)} fusion(bf16[4,16,32,16,227]{4,3,2,1,0:T(8,128)(2,1)} %get-tuple-element.202, s32[]{:T(128)} %get-tuple-element.201, bf16[16,128,16,227]{3,2,1,0:T(8,128)(2,1)} %get-tuple-element.215, s32[]{:T(128)S(6)} %select_n.18, f32[16,32,16,512]{3,2,1,0:T(8,128)} %fusion.96, ...), kind=kOutput, calls=%fused_computation.12.clone.1 | convolution fusion | flops 3855949824 | bytes 29836800 | tf_op jit(solution)/shard_map/while/body/eval_jaxpr/mijf,fc->mijc/dot_general | solution.py:27
  172.7 0.6 dynamic_slice.34
  174.0 10.3 %fusion.96 = f32[16,32,16,512]{3,2,1,0:T(8,128)} fusion(bf16[16,128,16,227]{3,2,1,0:T(8,128)(2,1)} %get-tuple-element.215, s32[]{:T(128)S(6)} %select_n.18, bf16[454,512]{1,0:T(8,128)(2,1)} %get-tuple-element.216), kind=kOutput, calls=%fused_computation.14.clone.1 | convolution fusion | flops 1904214016 | bytes 21209092 | tf_op jit(solution)/shard_map/while/body/eval_jaxpr/mijc,cf->mijf/dot_general | solution.py:24
  184.2 13.3 %fusion.97 = bf16[4,16,32,16,227]{4,3,2,1,0:T(8,128)(2,1)} fusion(bf16[4,16,32,16,227]{4,3,2,1,0:T(8,128)(2,1)} %get-tuple-element.202, s32[]{:T(128)} %get-tuple-element.201, bf16[16,128,16,227]{3,2,1,0:T(8,128)(2,1)} %get-tuple-element.215, s32[]{:T(128)S(6)} %select_n.18, f32[16,32,16,512]{3,2,1,0:T(8,128)} %fusion.96, ...), kind=kOutput, calls=%fused_computation.12.clone.1 | convolution fusion | flops 3855949824 | bytes 29836800 | tf_op jit(solution)/shard_map/while/body/eval_jaxpr/mijf,fc->mijc/dot_general | solution.py:27
  197.5 0.6 dynamic_slice.34
  198.8 10.3 %fusion.96 = f32[16,32,16,512]{3,2,1,0:T(8,128)} fusion(bf16[16,128,16,227]{3,2,1,0:T(8,128)(2,1)} %get-tuple-element.215, s32[]{:T(128)S(6)} %select_n.18, bf16[454,512]{1,0:T(8,128)(2,1)} %get-tuple-element.216), kind=kOutput, calls=%fused_computation.14.clone.1 | convolution fusion | flops 1904214016 | bytes 21209092 | tf_op jit(solution)/shard_map/while/body/eval_jaxpr/mijc,cf->mijf/dot_general | solution.py:24
  209.0 13.3 %fusion.97 = bf16[4,16,32,16,227]{4,3,2,1,0:T(8,128)(2,1)} fusion(bf16[4,16,32,16,227]{4,3,2,1,0:T(8,128)(2,1)} %get-tuple-element.202, s32[]{:T(128)} %get-tuple-element.201, bf16[16,128,16,227]{3,2,1,0:T(8,128)(2,1)} %get-tuple-element.215, s32[]{:T(128)S(6)} %select_n.18, f32[16,32,16,512]{3,2,1,0:T(8,128)} %fusion.96, ...), kind=kOutput, calls=%fused_computation.12.clone.1 | convolution fusion | flops 3855949824 | bytes 29836800 | tf_op jit(solution)/shard_map/while/body/eval_jaxpr/mijf,fc->mijc/dot_general | solution.py:27
  222.3 8.1 %all-to-all-start = ((bf16[4,16,32,16,227]{4,3,2,1,0:T(8,128)(2,1)}), bf16[4,16,32,16,227]{4,3,2,1,0:T(8,128)(2,1)}, u32[]{:S(2)}, u32[]{:S(2)}) async-start(bf16[4,16,32,16,227]{4,3,2,1,0:T(8,128)(2,1)} %get-tuple-element.64), calls=%async_computation | async-start | bytes 33554432 | tf_op jit(solution)/shard_map/all_to_all | solution.py:80
  230.5 181.8 %all-to-all-done = bf16[4,16,32,16,227]{4,3,2,1,0:T(8,128)(2,1)} async-done(((bf16[4,16,32,16,227]{4,3,2,1,0:T(8,128)(2,1)}), bf16[4,16,32,16,227]{4,3,2,1,0:T(8,128)(2,1)}, u32[]{:S(2)}, u32[]{:S(2)}) %all-to-all-start) | async-done | bytes 14876704 | tf_op jit(solution)/shard_map/all_to_all | solution.py:80
  412.3 12.1 %fusion.66 = (f32[8,4,16,32]{3,2,1,0:T(8,128)S(1)}, f32[64,8,4,16,32]{4,3,2,1,0:T(8,128)}) fusion(bf16[64,8,4,16,227]{4,3,2,1,0:T(8,128)(2,1)} %bitcast.9, bf16[227,32]{0,1:T(8,128)(2,1)S(1)} %copy-done.4), kind=kOutput, calls=%fused_computation.75 | convolution fusion | flops 477085696 | bytes 19151040 | tf_op jit(solution)/shard_map/kprqsc,co->kprqso/dot_general | solution.py:37
  424.4 18.1 %broadcast_multiply_fusion = (f32[64,8,4,16,32]{4,3,2,1,0:T(8,128)}, f32[64,8,4,16,32]{4,3,2,1,0:T(8,128)}) fusion(f32[8,4,16,32]{3,2,1,0:T(8,128)S(1)} %dynamic-slice_bitcast_fusion, f32[64,8,4,16,32]{4,3,2,1,0:T(8,128)} %get-tuple-element.125, f32[8,4,16,32]{3,2,1,0:T(8,128)S(1)} %broadcast_multiply_fusion.2), kind=kLoop, calls=%fused_computation.46 | loop fusion | flops 2097152 | bytes 12713984 | tf_op jit(solution)/shard_map/mul | solution.py:40
  442.5 14.2 %copy.40 = f32[64,8,4,16,32]{0,4,3,2,1:T(8,128)} copy(f32[64,8,4,16,32]{4,3,2,1,0:T(8,128)} %get-tuple-element.114) | data formatting | bytes 8388608 | tf_op jit(solution)/shard_map/mul | solution.py:40
  456.8 1.1 bitcast_subtract_fusion
  457.9 7.9 %convolution_bitcast_fusion.2 = f32[8,64,1]{1,2,0:T(1,128)S(1)} fusion(f32[64,8,4,16,32]{0,4,3,2,1:T(8,128)} %copy.40, f32[8,4,16,32,1]{3,4,2,1,0:T(1,128)S(1)} %bitcast.125), kind=kOutput, calls=%fused_computation.50 | convolution fusion | flops 12582912 | bytes 4261888 | tf_op jit(solution)/shard_map/kprqso,prqso->pqk/dot_general | solution.py:43
  465.8 40.2 %select_reduce_fusion = (f32[8]{0:T(128)S(1)}, f32[8,64,64]{2,1,0:T(8,128)S(1)}) fusion(pred[64,64]{1,0:T(8,128)(4,1)S(1)} %iota_compare_fusion.1, f32[64,8,4,16,32]{0,4,3,2,1:T(8,128)S(1)} %copy-done.2, f32[64,8,4,16,32]{4,3,2,1,0:T(8,128)} %get-tuple-element.115, f32[64,64]{1,0:T(8,128)S(1)} %fusion.58), kind=kOutput, calls=%fused_computation.58 | convolution fusion | flops 805404672 | bytes 8540192 | tf_op jit(solution)/shard_map/kprqso,lprqso->pqkl/dot_general | solution.py:42
  506.3 29.5 %while.24 = (s32[]{:T(128)}, f32[8,1,64,64]{2,3,0,1:T(8,128)S(1)}, f32[8,1,64,64]{3,2,0,1:T(8,128)S(1)}, s32[]{:T(128)}) while((s32[]{:T(128)}, f32[8,1,64,64]{2,3,0,1:T(8,128)S(1)}, f32[8,1,64,64]{3,2,0,1:T(8,128)S(1)}, s32[]{:T(128)}) %tuple.48), condition=%wide.region_6.7_spmd.clone, body=%wide.region_5.6_spmd.clone.sunk | while | flops 75571200 | bytes 1736757 | solution.py:52
  507.3 0.6 convolution_bitcast_fusion.5
  508.0 0.5 fusion.105
  509.0 0.6 convolution_bitcast_fusion.5
  510.6 0.6 convolution_bitcast_fusion.5
  511.3 0.5 fusion.105
  512.2 0.6 convolution_bitcast_fusion.5
  512.9 0.5 fusion.105
  513.9 0.6 convolution_bitcast_fusion.5
  515.5 0.6 convolution_bitcast_fusion.5
  516.2 0.5 fusion.105
  517.1 0.6 convolution_bitcast_fusion.5
  517.8 0.5 fusion.105
  518.8 0.6 convolution_bitcast_fusion.5
  519.5 0.5 fusion.105
  520.4 0.6 convolution_bitcast_fusion.5
  521.1 0.5 fusion.105
  522.1 0.6 convolution_bitcast_fusion.5
  523.7 0.6 convolution_bitcast_fusion.5
  524.4 0.5 fusion.105
  525.3 0.6 convolution_bitcast_fusion.5
  526.0 0.5 fusion.105
  527.0 0.6 convolution_bitcast_fusion.5
  528.6 0.6 convolution_bitcast_fusion.5
  530.3 0.6 convolution_bitcast_fusion.5
  531.9 0.6 convolution_bitcast_fusion.5
  532.6 0.5 fusion.105
  533.5 0.6 convolution_bitcast_fusion.5
  535.2 0.6 convolution_bitcast_fusion.5
  535.8 7.0 %convert_reduce_fusion = f32[32,16,227]{2,1,0:T(8,128)S(1)} fusion(bf16[4,16,32,16,227]{4,3,2,1,0:T(8,128)(2,1)} %all-to-all-done), kind=kLoop, calls=%fused_computation.42 | loop fusion | flops 14760448 | bytes 15341568 | tf_op jit(solution)/shard_map/reduce_sum | solution.py:35
  542.8 18.9 %convert_subtract_fusion = f32[64,8,4,16,227]{4,3,2,1,0:T(8,128)} fusion(bf16[64,8,4,16,227]{4,3,2,1,0:T(8,128)(2,1)} %bitcast.9, f32[8,4,16,227]{3,2,1,0:T(8,128)S(1)} %bitcast.123), kind=kLoop, calls=%fused_computation.41 | loop fusion | flops 14876672 | bytes 45094912 | tf_op jit(solution)/shard_map/sub | solution.py:36
  562.7 60.3 %fusion.37 = bf16[8,1,64,4,16,227]{5,2,4,3,0,1:T(8,128)(2,1)} fusion(f32[8,4,16,227]{3,2,1,0:T(8,128)S(1)} %bitcast.124, f32[64,8,4,16,227]{4,3,2,1,0:T(8,128)} %convert_subtract_fusion, f32[8,64]{1,0:T(8,128)S(1)} %bitcast.126, f32[8,1,64,64]{3,2,0,1:T(8,128)S(1)} %get-tuple-element.65, f32[8]{0:T(128)S(1)} %sqrt.8), kind=kOutput, calls=%fused_computation.38 | convolution fusion | flops 5727617024 | bytes 45228064 | tf_op jit(solution)/shard_map/kprqsc,pqke->prqsec/dot_general | solution.py:57
  (121 shorter events, 13.6 us)
Async XLA Ops:
  0.0 230.5 %copy-start = (f32[32,4,1,16,32]{4,3,2,1,0:T(8,128)S(1)}, f32[32,4,1,16,32]{4,3,2,1,0:T(8,128)}, u32[]{:S(2)}) copy-start(f32[32,4,1,16,32]{4,3,2,1,0:T(8,128)} %param.15) | copy-start | bytes 786436
  9.3 66.7 %collective-permute-start = (bf16[16,128,1,227]{1,0,3,2:T(8,128)(2,1)}, bf16[16,128,1,227]{1,0,3,2:T(8,128)(2,1)}, u32[]{:S(2)}, u32[]{:S(2)}) collective-permute-start(bf16[16,128,1,227]{1,0,3,2:T(8,128)(2,1)} %copy.60), channel_id=1, source_target_pairs={{0,4},{4,0},{1,5},{5,1},{2,6},{6,2},{3,7},{7,3}} | collective-permute-start | bytes 2789384 | tf_op jit(solution)/shard_map/ppermute | solution.py:72
  12.5 67.4 %collective-permute-start.1 = (bf16[16,128,1,227]{1,0,3,2:T(8,128)(2,1)}, bf16[16,128,1,227]{1,0,3,2:T(8,128)(2,1)}, u32[]{:S(2)}, u32[]{:S(2)}) collective-permute-start(bf16[16,128,1,227]{1,0,3,2:T(8,128)(2,1)} %copy.61), channel_id=1, source_target_pairs={{0,4},{4,0},{1,5},{5,1},{2,6},{6,2},{3,7},{7,3}} | collective-permute-start | bytes 2789384 | tf_op jit(solution)/shard_map/ppermute | solution.py:73
  37.4 26.5 %copy-start.1 = (bf16[16,128,16,227]{3,2,1,0:T(8,128)(2,1)S(1)}, bf16[16,128,16,227]{3,2,1,0:T(8,128)(2,1)}, u32[]{:S(2)}) copy-start(bf16[16,128,16,227]{3,2,1,0:T(8,128)(2,1)} %copy.39) | copy-start | bytes 44630020
  123.1 11.5 %copy-start.3 = (bf16[454,512]{1,0:T(8,128)(2,1)S(1)}, bf16[454,512]{1,0:T(8,128)(2,1)}, u32[]{:S(2)}) copy-start(bf16[454,512]{1,0:T(8,128)(2,1)} %get-tuple-element.216) | copy-start | bytes 1394692 | tf_op jit(solution)/shard_map/while
  123.1 11.5 %copy-start.5 = (bf16[512,227]{0,1:T(8,128)(2,1)S(1)}, bf16[512,227]{0,1:T(8,128)(2,1)}, u32[]{:S(2)}) copy-start(bf16[512,227]{0,1:T(8,128)(2,1)} %get-tuple-element.218) | copy-start | bytes 697348 | tf_op jit(solution)/shard_map/while
  147.9 11.5 %copy-start.3 = (bf16[454,512]{1,0:T(8,128)(2,1)S(1)}, bf16[454,512]{1,0:T(8,128)(2,1)}, u32[]{:S(2)}) copy-start(bf16[454,512]{1,0:T(8,128)(2,1)} %get-tuple-element.216) | copy-start | bytes 1394692 | tf_op jit(solution)/shard_map/while
  147.9 11.5 %copy-start.5 = (bf16[512,227]{0,1:T(8,128)(2,1)S(1)}, bf16[512,227]{0,1:T(8,128)(2,1)}, u32[]{:S(2)}) copy-start(bf16[512,227]{0,1:T(8,128)(2,1)} %get-tuple-element.218) | copy-start | bytes 697348 | tf_op jit(solution)/shard_map/while
  172.7 11.5 %copy-start.3 = (bf16[454,512]{1,0:T(8,128)(2,1)S(1)}, bf16[454,512]{1,0:T(8,128)(2,1)}, u32[]{:S(2)}) copy-start(bf16[454,512]{1,0:T(8,128)(2,1)} %get-tuple-element.216) | copy-start | bytes 1394692 | tf_op jit(solution)/shard_map/while
  172.7 11.5 %copy-start.5 = (bf16[512,227]{0,1:T(8,128)(2,1)S(1)}, bf16[512,227]{0,1:T(8,128)(2,1)}, u32[]{:S(2)}) copy-start(bf16[512,227]{0,1:T(8,128)(2,1)} %get-tuple-element.218) | copy-start | bytes 697348 | tf_op jit(solution)/shard_map/while
  197.5 11.5 %copy-start.3 = (bf16[454,512]{1,0:T(8,128)(2,1)S(1)}, bf16[454,512]{1,0:T(8,128)(2,1)}, u32[]{:S(2)}) copy-start(bf16[454,512]{1,0:T(8,128)(2,1)} %get-tuple-element.216) | copy-start | bytes 1394692 | tf_op jit(solution)/shard_map/while
  197.5 11.5 %copy-start.5 = (bf16[512,227]{0,1:T(8,128)(2,1)S(1)}, bf16[512,227]{0,1:T(8,128)(2,1)}, u32[]{:S(2)}) copy-start(bf16[512,227]{0,1:T(8,128)(2,1)} %get-tuple-element.218) | copy-start | bytes 697348 | tf_op jit(solution)/shard_map/while
  222.3 190.0 %copy-start.4 = (bf16[227,32]{0,1:T(8,128)(2,1)S(1)}, bf16[227,32]{0,1:T(8,128)(2,1)}, u32[]{:S(2)}) copy-start(bf16[227,32]{0,1:T(8,128)(2,1)} %param.13) | copy-start | bytes 43588
  222.3 190.0 %all-to-all-start = ((bf16[4,16,32,16,227]{4,3,2,1,0:T(8,128)(2,1)}), bf16[4,16,32,16,227]{4,3,2,1,0:T(8,128)(2,1)}, u32[]{:S(2)}, u32[]{:S(2)}) async-start(bf16[4,16,32,16,227]{4,3,2,1,0:T(8,128)(2,1)} %get-tuple-element.64), calls=%async_computation | async-start | bytes 33554432 | tf_op jit(solution)/shard_map/all_to_all | solution.py:80
  456.8 9.0 %copy-start.2 = (f32[64,8,4,16,32]{0,4,3,2,1:T(8,128)S(1)}, f32[64,8,4,16,32]{0,4,3,2,1:T(8,128)}, u32[]{:S(2)}) copy-start(f32[64,8,4,16,32]{0,4,3,2,1:T(8,128)} %copy.40) | copy-start | bytes 12582916
where the time goes:
time: 633 us; the launch traced here: 623 us
  matrix products  243 us (38%)
  waiting for transfers between devices  182 us (29%)
  local copies, waits for them, and re-layouts  99.8 us (16%)
  other arithmetic  84 us (13%)
  starting transfers between devices  10.2 us (2%)
    all_to_all x1, waiting for transfers between devices, local_step(): received = lax.all_to_all(fc_blocks, 'ens', 0, 0, tiled=True)  182 us
    dot_general x1, matrix products, patch_analysis(): jnp.einsum('kprqsc,pqke->prqsec', anomaly, transform, precision=FULL_PREC...  60.3 us
    dot_general x4, matrix products, value_a13(): jnp.einsum('mijf,fc->mijc', gelu_out, w_out, preferred_element_type=jnp.f...  53.1 us
    dot_general x4, matrix products, value_a13(): jnp.einsum('mijc,cf->mijf', state_blk, w_in[:channels], preferred_element...  41.1 us
    dot_general x1, matrix products, patch_analysis(): jnp.einsum('kprqso,lprqso->pqkl', weighted, obs_anom, precision=FULL_PREC...  40.2 us
    convert_element_type x1, other arithmetic, five_point(): return total.astype(jnp.bfloat16)  38.6 us
    slice x1, local copies, waits for them, and re-layouts, five_point(): ens_state[:, :, 1:]  26.4 us
    while x1, local copies, waits for them, and re-layouts, local_step(): fc_blocks = lax.map(value_a14, jnp.arange(ens_size))  24.9 us
  transfers between devices with their start and end apart: 3, of which 1 were waited for; matrix products, arithmetic and copies ran while one was open for 11% of the time, Pallas kernels for 0%

commit v1 on v0

v1 whole, which is shorter than its diff:
```python
import functools
import math
import jax
import jax.numpy as jnp
from jax import lax
from jax.experimental import pallas as pl
from jax.experimental.pallas import tpu as pltpu
from jax.sharding import PartitionSpec as P

NS_STEPS = 18
MESH = pl.DeviceIdType.MESH
CP = 256
NT = (((1,), (1,)), ((), ()))


NN = (((1,), (0,)), ((), ()))


def split3(a):
    hi = a.astype(jnp.bfloat16)
    rem = a - hi.astype(jnp.float32)
    mid = rem.astype(jnp.bfloat16)
    low = (rem - mid.astype(jnp.float32)).astype(jnp.bfloat16)
    return hi, mid, low


def f32dot(a, b, dims=NN):
    ah, am, al = split3(a)
    bh, bm, bl = split3(b)
    n = a.shape[0]

    def dot(u, v):
        return lax.dot_general(u, v, dims, preferred_element_type=jnp.float32)
    by_hi = dot(jnp.concatenate([ah, am, al], axis=0), bh)
    by_mid = dot(jnp.concatenate([ah, am], axis=0), bm)
    by_low = dot(ah, bl)
    small = (by_low + by_hi[2 * n:]) + by_mid[n:]
    return (small + (by_mid[:n] + by_hi[n:2 * n])) + by_hi[:n]


def exchange_kernel(dims, x_hbm, wi_ref, wo_ref, op_ref, yo_ref, wt_ref, g_hbm, tt_ref,
                    xv, xs, xl, ts, sb, gath, gsend, grecv, wobs, yp, cm,
                    xsem, gssem, grsem, ssem, rsem, gsem):
    members, rows, columns, channels, patches, dev_rows, ens_size = dims
    rest = channels - 128
    units = patches * ens_size
    total_m = members * ens_size
    me = lax.axis_index("ens")
    mydom = lax.axis_index("dom")
    my_x, my_core = me // 2, me % 2

    def dest_of(dslot):
        dx = (my_x + 1 - dslot // 2) % 2
        dc = (my_core + (dslot + 1) // 2) % 2
        return dx * 2 + dc

    barrier = pltpu.get_barrier_semaphore()
    for dslot in range(3):
        pl.semaphore_signal(barrier, inc=1, device_id={"ens": dest_of(dslot)}, device_id_type=MESH)
    pl.semaphore_signal(barrier, inc=1, device_id={"dom": 1 - mydom}, device_id_type=MESH)
    pl.semaphore_wait(barrier, 4)

    def x_copies(unit, action):
        patch, dslot = unit // ens_size, unit % ens_size
        slot = unit % 2
        first = dest_of(dslot) * dev_rows + patch * 4
        north = jnp.maximum(first - 1, 0)
        south = jnp.minimum(first + 4, rows - 1)
        for idx, (src, num, dst) in enumerate(((first, 4, 1), (north, 1, 0), (south, 1, 5))):
            copy = pltpu.make_async_copy(x_hbm.at[:, pl.ds(src, num)], xv.at[slot, :, pl.ds(dst, num)], xsem.at[slot, idx])
            action(copy)

    def ghost_copy(unit):
        return pltpu.make_async_remote_copy(
            src_ref=gsend.at[unit], dst_ref=grecv.at[unit], send_sem=gssem.at[unit], recv_sem=grsem.at[unit],
            device_id={"dom": 1 - mydom}, device_id_type=MESH)

    def unit_copy(patch, dslot):
        return pltpu.make_async_remote_copy(
            src_ref=sb.at[patch * 3 + dslot], dst_ref=gath.at[patch, :, :, pl.ds(me * members, members)],
            send_sem=ssem.at[patch, dslot], recv_sem=rsem.at[patch, dslot],
            device_id={"ens": dest_of(dslot)}, device_id_type=MESH)

    def gath_copy(patch):
        return pltpu.make_async_copy(gath.at[patch], g_hbm.at[patch], gsem.at[patch])

    x_copies(0, lambda c: c.start())

    xs[...] = jnp.zeros_like(xs)
    wobs[...] = jnp.zeros_like(wobs)
    for j in range(8):
        place = (lax.broadcasted_iota(jnp.int32, (32, CP), 1) == lax.broadcasted_iota(jnp.int32, (32, CP), 0) + 32 * j)
        wobs[j * CP:(j + 1) * CP, :] = jnp.dot(op_ref[...], place.astype(jnp.bfloat16), preferred_element_type=jnp.float32).astype(jnp.bfloat16)

    def prepare(unit):
        slot = unit % 2

        @pl.when(unit + 1 < units)
        def _():
            x_copies(unit + 1, lambda c: c.start())
        x_copies(unit, lambda c: c.wait())

        def convert(r, carry):
            for m in range(members):
                v = xv[slot, m, r]
                xs[slot, 0, r, 32 * m + 8:32 * m + 24, :] = v[:, :128].astype(jnp.float32)
                xs[slot, 1, r, 32 * m + 8:32 * m + 24, 0:rest] = v[:, 128:].astype(jnp.float32)
            return carry
        lax.fori_loop(0, 6, convert, 0)

        def edges(r, carry):
            for h in range(2):
                gsend[unit, 0, r, :, h * 128:h * 128 + 128] = xs[slot, h, r + 1, pl.ds(23, members, stride=32), :].astype(jnp.bfloat16)
                gsend[unit, 1, r, :, h * 128:h * 128 + 128] = xs[slot, h, r + 1, pl.ds(8, members, stride=32), :].astype(jnp.bfloat16)
            return carry
        lax.fori_loop(0, 4, edges, 0)
        ghost_copy(unit).start()

    def forecast(unit):
        patch, dslot = unit // ens_size, unit % ens_size
        slot = unit % 2
        out_slot = jnp.where(dslot < 3, patch * 3 + dslot, patches * 3)
        ghost_copy(unit).wait_recv()

        def block(r, carry):
            for h in range(2):
                xs[slot, h, r + 1, pl.ds(7, members, stride=32), :] = grecv[unit, 0, r, :, h * 128:h * 128 + 128].astype(jnp.float32)
                xs[slot, h, r + 1, pl.ds(24, members, stride=32), :] = grecv[unit, 1, r, :, h * 128:h * 128 + 128].astype(jnp.float32)
            for m in range(members):
                b = 32 * m
                for h in range(2):
                    cur = xs[slot, h, r + 1, b + 8:b + 24, :]
                    north = xs[slot, h, r, b + 8:b + 24, :]
                    south = xs[slot, h, r + 2, b + 8:b + 24, :]
                    west = xs[slot, h, r + 1, b + 7:b + 23, :]
                    east = xs[slot, h, r + 1, b + 9:b + 25, :]
                    lap = north + south + west + east - 4.0 * cur
                    xl[16 * m:16 * m + 16, h * 128:h * 128 + 128] = cur.astype(jnp.bfloat16)
                    xl[16 * m:16 * m + 16, CP + h * 128:CP + h * 128 + 128] = lap.astype(jnp.bfloat16)
            hidden = jnp.dot(xl[...], wi_ref[...], preferred_element_type=jnp.float32)
            gel = jax.nn.gelu(hidden, approximate=True).astype(jnp.bfloat16)
            inc = jnp.dot(gel, wo_ref[...], preferred_element_type=jnp.float32)
            for m in range(members):
                for h in range(2):
                    ts[h, 16 * m:16 * m + 16, :] = xs[slot, h, r + 1, 32 * m + 8:32 * m + 24, :] + inc[16 * m:16 * m + 16, h * 128:h * 128 + 128]
            for col in range(columns):
                for h in range(2):
                    sb[out_slot, r, col, :, h * 128:h * 128 + 128] = ts[h, pl.ds(col, members, stride=16), :].astype(jnp.bfloat16)
            return carry
        lax.fori_loop(0, 4, block, 0)

        @pl.when(dslot < 3)
        def _():
            unit_copy(patch, dslot).start()

        @pl.when(dslot == 3)
        def _():
            def own(r, carry):
                gath[patch, r, :, pl.ds(pl.multiple_of(me * members, members), members), :] = sb[patches * 3, r]
                return carry
            lax.fori_loop(0, 4, own, 0)

    def analysis(patch):
        for dslot in range(3):
            unit_copy(patch, dslot).wait_recv()
        gath_copy(patch).start()
        eye = (lax.broadcasted_iota(jnp.int32, (total_m, total_m), 0) == lax.broadcasted_iota(jnp.int32, (total_m, total_m), 1)).astype(jnp.float32)
        csum = jnp.zeros((total_m, CP), jnp.float32)
        for half in range(2):
            lhs = jnp.concatenate([gath[patch, :, half * 8 + j].reshape(4 * total_m, CP) for j in range(8)], axis=1)
            yb = jnp.dot(lhs, wobs[...], preferred_element_type=jnp.float32)
            for r in range(4):
                g = half * 4 + r
                y = yb[r * total_m:(r + 1) * total_m]
                ybar = jnp.sum(y, axis=0, keepdims=True) * (1.0 / total_m)
                y = y - ybar
                c = y * wt_ref[patch, g:g + 1, :]
                csum = csum + c * (yo_ref[patch, g:g + 1, :] - ybar)
                yp[g] = y
                cm[g] = c
        a_mat = (total_m - 1.0) * eye
        for g in range(8):
            a_mat = a_mat + f32dot(cm[g], yp[g], NT)
        trace = jnp.sum(jnp.sum(a_mat * eye, axis=0, keepdims=True), axis=1, keepdims=True)

        def newton(step, carry):
            y, z = carry
            mix = 1.5 * eye - 0.5 * f32dot(z, y)
            return f32dot(y, mix), f32dot(mix, z)
        _, inv = lax.fori_loop(0, NS_STEPS, newton, (a_mat / trace, eye))
        root = inv / jnp.sqrt(trace)
        rhs = jnp.broadcast_to(jnp.sum(csum, axis=1, keepdims=True), (total_m, total_m))
        wbar = f32dot(root, f32dot(root, rhs))
        trans = math.sqrt(total_m - 1.0) * root + wbar
        trans = trans + (1.0 - jnp.sum(trans, axis=0, keepdims=True)) * (1.0 / total_m)
        tt_ref[patch] = trans.T

    def step(v, carry):
        @pl.when(v < units)
        def _():
            prepare(v)

        @pl.when((v >= 1) & (v <= units))
        def _():
            forecast(v - 1)

        @pl.when((v >= 12) & (v % 4 == 0))
        def _():
            analysis(v // 4 - 3)
        return carry
    lax.fori_loop(0, units + 9, step, 0)

    def finish(patch, carry):
        for dslot in range(3):
            unit_copy(patch, dslot).wait_send()
        for dslot in range(4):
            ghost_copy(patch * 4 + dslot).wait_send()
        gath_copy(patch).wait()
        return carry
    lax.fori_loop(0, patches, finish, 0)


def update_kernel(tt_ref, g_ref, out_ref):
    t = tt_ref[0]
    hi = t.astype(jnp.bfloat16)
    r1 = t - hi.astype(jnp.float32)
    mid = r1.astype(jnp.bfloat16)
    low = (r1 - mid.astype(jnp.float32)).astype(jnp.bfloat16)
    lhs = jnp.concatenate([hi, mid, low], axis=0)
    n = t.shape[0]
    for col in range(g_ref.shape[2]):
        res = jnp.dot(lhs, g_ref[0, 0, col], preferred_element_type=jnp.float32)
        val = (res[2 * n:] + res[n:2 * n]) + res[:n]
        out_ref[0, col] = val[:, :out_ref.shape[3]].astype(jnp.bfloat16)


def solution(mesh):
    ens_size = mesh.shape["ens"]
    obs_spec = P(None, None, "dom", None, None)

    def local_step(ens_state, w_in, w_out, obs_op, obs_val, obs_wt):
        members, rows, columns, channels = ens_state.shape
        hidden = w_in.shape[1]
        total_m = members * ens_size
        dev_rows = rows // ens_size
        patches = dev_rows // 4
        units = patches * ens_size
        obs = obs_op.shape[1]
        pad = ((0, CP - channels), (0, 0))
        wi = jnp.concatenate([jnp.pad(w_in[:channels], pad), jnp.pad(w_in[channels:], pad)], axis=0)
        wo = jnp.pad(w_out, ((0, 0), (0, CP - channels)))
        op = jnp.pad(obs_op, pad)
        start = lax.axis_index("ens") * patches

        def arrange(v):
            v = lax.dynamic_slice_in_dim(v, start, patches, axis=0)
            v = v.reshape(patches, 4, 2, 8 * obs).transpose(0, 2, 1, 3)
            return v.reshape(patches, 8, 8 * obs)
        yo, wt = arrange(obs_val), arrange(obs_wt)
        dims = (members, rows, columns, channels, patches, dev_rows, ens_size)
        vmem = pl.BlockSpec(memory_space=pltpu.VMEM)
        anym = pl.BlockSpec(memory_space=pl.ANY)
        bf, f32 = jnp.bfloat16, jnp.float32
        dma = pltpu.SemaphoreType.DMA
        gathered, trans = pl.pallas_call(
            functools.partial(exchange_kernel, dims),
            out_shape=(jax.ShapeDtypeStruct((patches, 4, columns, total_m, CP), bf),
                       jax.ShapeDtypeStruct((patches, total_m, total_m), f32)),
            in_specs=[anym, vmem, vmem, vmem, vmem, vmem],
            out_specs=(anym, vmem),
            scratch_shapes=[
                pltpu.VMEM((2, members, 6, columns, channels), bf),
                pltpu.VMEM((2, 2, 6, members * 32, 128), f32),
                pltpu.VMEM((members * columns, 2 * CP), bf),
                pltpu.VMEM((2, members * columns, 128), f32),
                pltpu.VMEM((patches * 3 + 1, 4, columns, members, CP), bf),
                pltpu.VMEM((patches, 4, columns, total_m, CP), bf),
                pltpu.VMEM((units, 2, 4, members, CP), bf),
                pltpu.VMEM((units, 2, 4, members, CP), bf),
                pltpu.VMEM((8 * CP, CP), bf),
                pltpu.VMEM((8, total_m, CP), f32),
                pltpu.VMEM((8, total_m, CP), f32),
                dma((2, 3)), dma((units,)), dma((units,)), dma((patches, 3)), dma((patches, 3)), dma((patches,)),
            ],
            compiler_params=pltpu.CompilerParams(collective_id=0, has_side_effects=True, vmem_limit_bytes=62 * 1024 * 1024),
        )(ens_state, wi, wo, op, yo, wt)
        return pl.pallas_call(
            update_kernel,
            grid=(patches, 4),
            out_shape=jax.ShapeDtypeStruct((dev_rows, columns, total_m, channels), bf),
            in_specs=[pl.BlockSpec((1, total_m, total_m), lambda p, r: (p, 0, 0)),
                      pl.BlockSpec((1, 1, columns, total_m, CP), lambda p, r: (p, r, 0, 0, 0))],
            out_specs=pl.BlockSpec((1, columns, total_m, channels), lambda p, r: (p * 4 + r, 0, 0, 0)),
            compiler_params=pltpu.CompilerParams(dimension_semantics=("arbitrary", "arbitrary")),
        )(trans, gathered)

    return jax.shard_map(local_step, mesh=mesh, in_specs=(P("ens", None, "dom", None), P(), P(), P(), obs_spec, obs_spec), out_specs=P("ens", "dom", None, None), check_vma=False)
```

time: 633 us -> 268 us (0.42); the launches traced: 623 us -> 266 us
  matrix products: 243 us -> 0 us
  Pallas kernels: 0 us -> 233 us
  waiting for transfers between devices: 182 us -> 0 us
  other arithmetic: 84 us -> 1.87 us
  local copies, waits for them, and re-layouts: 99.8 us -> 31.8 us
  starting transfers between devices: 10.2 us -> 0 us
    dot_general x68 -> x0, matrix products: 243 us -> none  [the longest x1 60.3 us: patch_analysis(): jnp.einsum('kprqsc,pqke->prqsec', anomaly, transform, precision=FULL_PREC...]
    pallas_call x0 -> x2, Pallas kernels: none -> 233 us  [the longest x1 202 us: local_step(): pl.pallas_call(functools.partial(exchange_kernel, dims), out_shape=(jax.S...]
    all_to_all x1 -> x0, waiting for transfers between devices: 182 us -> none  [local_step(): received = lax.all_to_all(fc_blocks, 'ens', 0, 0, tiled=True)]
    slice x4 -> x1, local copies, waits for them, and re-layouts: 46.8 us -> 1 us  [local_step(): w_in[channels:]]
    convert_element_type x2 -> x0, other arithmetic: 38.6 us -> none  [the longest x1 38.6 us: five_point(): return total.astype(jnp.bfloat16)]
    while x53 -> x0, local copies, waits for them, and re-layouts: 25.6 us -> none  [the longest x1 24.9 us: local_step(): fc_blocks = lax.map(value_a14, jnp.arange(ens_size))]
    unnamed x11 -> x3, local copies, waits for them, and re-layouts: 2.38 us -> 26.7 us
    sub x2 -> x0, other arithmetic: 20.1 us -> none  [the longest x1 18.9 us: patch_analysis(): anomaly = fc_tiles.astype(jnp.float32) - mean_fc]
  transfers between devices with their start and end apart: 3 -> 0, of which waited for: 1 -> 0; matrix products, arithmetic and copies ran while one was open for 11% -> 0% of each run, Pallas kernels for 0% -> 0%
where the time goes in v1:
time: 268 us; the launch traced here: 266 us
  Pallas kernels  233 us (87%)
  local copies, waits for them, and re-layouts  31.8 us (12%)
    pallas_call x1, Pallas kernels, local_step(): pl.pallas_call(functools.partial(exchange_kernel, dims), out_shape=(jax.S...  202 us
    pallas_call x1, Pallas kernels, local_step(): pl.pallas_call(update_kernel, grid=(patches, 4), out_shape=jax.ShapeDtype...  30.4 us
    unnamed x3, local copies, waits for them, and re-layouts  26.7 us

profile of v1, /device:TPU:1, one launch (start us, length us, event | category | flops | bytes accessed | tf_op | source)
XLA Modules:
  0.0 266.4 jit_solution(11826613162853838369)
XLA Ops:
  0.0 0.8 copy.11
  0.8 0.7 pad.18.op_ref
  1.5 1.0 slice.8
  2.5 1.1 copy.10
  3.6 0.7 pad.17.wo_ref
  4.3 1.1 slice_select_fusion
  5.4 0.8 fusion.1.wi_ref
  6.2 1.1 constant_dynamic-slice_fusion
  7.2 0.1 reshape.14
  7.4 0.6 reshape.15.wt_ref
  8.1 0.1 reshape.12
  8.2 0.6 reshape.13.yo_ref
  8.9 24.8 %copy.14.x_hbm = bf16[16,128,16,227]{3,2,1,0:T(8,128)(2,1)} copy(bf16[16,128,16,227]{1,2,3,0:T(8,128)(2,1)} %param.6) | data formatting | bytes 29753344 | tf_op args[0]
  33.7 202.3 %shard_map.64 = (bf16[8,4,16,64,256]{4,3,2,1,0:T(8,128)(2,1)}, f32[8,64,64]{2,1,0:T(8,128)}) custom-call(bf16[16,128,16,227]{3,2,1,0:T(8,128)(2,1)} %copy.14.x_hbm, bf16[512,512]{1,0:T(8,128)(2,1)} %fusion.1.wi_ref, bf16[512,256]{1,0:T(8,128)(2,1)} %pad.17.wo_ref, bf16[256,32]{1,0:T(8,128)(2,1)} %pad.18.op_ref, f32[8,8,256]{2,1,0:T(8,128)} %reshape.13.yo_ref, ...), custom_call_target="tpu_custom_call" | custom-call | tf_op jit(solution)/shard_map/pallas_call | solution.py:265
  236.1 30.4 %shard_map.65 = bf16[32,16,64,227]{3,2,1,0:T(8,128)(2,1)} custom-call(f32[8,64,64]{2,1,0:T(8,128)} %get-tuple-element.7.tt_ref, bf16[8,4,16,64,256]{4,3,2,1,0:T(8,128)(2,1)} %get-tuple-element.8.g_ref), custom_call_target="tpu_custom_call" | custom-call | tf_op jit(solution)/shard_map/pallas_call | solution.py:287
  (2 shorter events, 0.0 us)

commit v2 on v1

--- a/solution.py
+++ b/solution.py
@@ -38,9 +38,9 @@
     return (small + (by_mid[:n] + by_hi[n:2 * n])) + by_hi[:n]
 
 
-def exchange_kernel(dims, x_hbm, wi_ref, wo_ref, op_ref, yo_ref, wt_ref, g_hbm, tt_ref,
-                    xv, xs, xl, ts, sb, gath, gsend, grecv, wobs, yp, cm,
-                    xsem, gssem, grsem, ssem, rsem, gsem):
+def exchange_kernel(dims, x_hbm, wi_ref, wo_ref, op_ref, yo_hbm, wt_hbm, g_hbm, tt_ref,
+                    xv, xs, xl, ts, t2, sb1, sb2, rb, gath, gsend, grecv, wi, wo, wf, wobs, obs_raw, obs_row, yp, cm,
+                    xsem, gssem, grsem, ssem, rsem, gsem, osem):
     members, rows, columns, channels, patches, dev_rows, ens_size = dims
     rest = channels - 128
     units = patches * ens_size
@@ -48,17 +48,12 @@
     me = lax.axis_index("ens")
     mydom = lax.axis_index("dom")
     my_x, my_core = me // 2, me % 2
+    mine = pl.ds(pl.multiple_of(me * members, members), members)
 
     def dest_of(dslot):
         dx = (my_x + 1 - dslot // 2) % 2
         dc = (my_core + (dslot + 1) // 2) % 2
         return dx * 2 + dc
-
-    barrier = pltpu.get_barrier_semaphore()
-    for dslot in range(3):
-        pl.semaphore_signal(barrier, inc=1, device_id={"ens": dest_of(dslot)}, device_id_type=MESH)
-    pl.semaphore_signal(barrier, inc=1, device_id={"dom": 1 - mydom}, device_id_type=MESH)
-    pl.semaphore_wait(barrier, 4)
 
     def x_copies(unit, action):
         patch, dslot = unit // ens_size, unit % ens_size
@@ -75,22 +70,67 @@
             src_ref=gsend.at[unit], dst_ref=grecv.at[unit], send_sem=gssem.at[unit], recv_sem=grsem.at[unit],
             device_id={"dom": 1 - mydom}, device_id_type=MESH)
 
-    def unit_copy(patch, dslot):
-        return pltpu.make_async_remote_copy(
-            src_ref=sb.at[patch * 3 + dslot], dst_ref=gath.at[patch, :, :, pl.ds(me * members, members)],
-            send_sem=ssem.at[patch, dslot], recv_sem=rsem.at[patch, dslot],
-            device_id={"ens": dest_of(dslot)}, device_id_type=MESH)
+    def unit_copies(patch, dslot):
+        dev = {"ens": dest_of(dslot)}
+        first = pltpu.make_async_remote_copy(
+            src_ref=sb1.at[patch * 3 + dslot], dst_ref=gath.at[patch, :, :, mine, pl.ds(0, 128)],
+            send_sem=ssem.at[patch, dslot, 0], recv_sem=rsem.at[patch, dslot, 0],
+            device_id=dev, device_id_type=MESH)
+        second = pltpu.make_async_remote_copy(
+            src_ref=sb2.at[patch * 3 + dslot], dst_ref=rb.at[patch * 3 + dslot],
+            send_sem=ssem.at[patch, dslot, 1], recv_sem=rsem.at[patch, dslot, 1],
+            device_id=dev, device_id_type=MESH)
+        return first, second
 
     def gath_copy(patch):
         return pltpu.make_async_copy(gath.at[patch], g_hbm.at[patch], gsem.at[patch])
 
+    obs_copies = [pltpu.make_async_copy(ref.at[pl.ds(me * patches, patches)], obs_raw.at[i], osem.at[i]) for i, ref in enumerate((yo_hbm, wt_hbm))]
+
     x_copies(0, lambda c: c.start())
-
-    xs[...] = jnp.zeros_like(xs)
-    wobs[...] = jnp.zeros_like(wobs)
-    for j in range(8):
-        place = (lax.broadcasted_iota(jnp.int32, (32, CP), 1) == lax.broadcasted_iota(jnp.int32, (32, CP), 0) + 32 * j)
-        wobs[j * CP:(j + 1) * CP, :] = jnp.dot(op_ref[...], place.astype(jnp.bfloat16), preferred_element_type=jnp.float32).astype(jnp.bfloat16)
+    for copy in obs_copies:
+        copy.start()
+    barrier = pltpu.get_barrier_semaphore()
+    for dslot in range(3):
+        pl.semaphore_signal(barrier, inc=1, device_id={"ens": dest_of(dslot)}, device_id_type=MESH)
+    pl.semaphore_signal(barrier, inc=1, device_id={"dom": 1 - mydom}, device_id_type=MESH)
+
+    xs[:, 1] = jnp.zeros((2, 6, members * 32, 128), jnp.float32)
+    wf[...] = jnp.zeros_like(wf)
+    wf[0:channels, :] = wo_ref[...].astype(jnp.float32)
+    wo[...] = wf[0:CP, :].T.astype(jnp.bfloat16)
+    wf[0:2 * channels, :] = wi_ref[...].astype(jnp.float32)
+    keep = lax.broadcasted_iota(jnp.int32, (CP, 512), 0) < channels
+    wi[0:CP, :] = jnp.where(keep, wf[0:CP, :], 0.0).astype(jnp.bfloat16)
+    wi[CP:2 * CP, :] = wf[channels:channels + CP, :].astype(jnp.bfloat16)
+    pl.semaphore_wait(barrier, 4)
+
+    lane = lax.broadcasted_iota(jnp.int32, (members, 128), 1)
+
+    def setup():
+        wf[0:128, 0:CP] = jnp.zeros((128, CP), jnp.float32)
+        wf[0:32, 0:channels] = op_ref[...].astype(jnp.float32)
+        opt = wf[0:128, 0:CP].T.astype(jnp.bfloat16)
+        for j in range(8):
+            place = (lax.broadcasted_iota(jnp.int32, (128, CP), 1) == lax.broadcasted_iota(jnp.int32, (128, CP), 0) + 32 * j)
+            wobs[j * CP:(j + 1) * CP, :] = jnp.dot(opt, place.astype(jnp.bfloat16), preferred_element_type=jnp.float32).astype(jnp.bfloat16)
+        for copy in obs_copies:
+            copy.wait()
+        sub8 = lax.broadcasted_iota(jnp.int32, (8, 128), 0)
+        lane8 = lax.broadcasted_iota(jnp.int32, (8, 128), 1) // 32
+        wf[0:8, 0:128] = jnp.zeros((8, 128), jnp.float32)
+
+        def rows_of(patch, carry):
+            for i in range(2):
+                for g in range(8):
+                    wf[0:8, 0:32] = obs_raw[i, patch, g % 4, 0, (g // 4) * 8:(g // 4) * 8 + 8, :]
+                    v = wf[0:8, 0:128]
+                    v = v + pltpu.roll(v, 32, 1)
+                    v = v + pltpu.roll(v, 64, 1)
+                    for q in range(2):
+                        obs_row[i, patch, g:g + 1, q * 128:q * 128 + 128] = jnp.sum(jnp.where(sub8 == lane8 + 4 * q, v, 0.0), axis=0, keepdims=True)
+            return carry
+        lax.fori_loop(0, patches, rows_of, 0)
 
     def prepare(unit):
         slot = unit % 2
@@ -137,32 +177,69 @@
                     lap = north + south + west + east - 4.0 * cur
                     xl[16 * m:16 * m + 16, h * 128:h * 128 + 128] = cur.astype(jnp.bfloat16)
                     xl[16 * m:16 * m + 16, CP + h * 128:CP + h * 128 + 128] = lap.astype(jnp.bfloat16)
-            hidden = jnp.dot(xl[...], wi_ref[...], preferred_element_type=jnp.float32)
+            hidden = jnp.dot(xl[...], wi[...], preferred_element_type=jnp.float32)
             gel = jax.nn.gelu(hidden, approximate=True).astype(jnp.bfloat16)
-            inc = jnp.dot(gel, wo_ref[...], preferred_element_type=jnp.float32)
+            inc = jnp.dot(gel, wo[...], preferred_element_type=jnp.float32)
             for m in range(members):
                 for h in range(2):
                     ts[h, 16 * m:16 * m + 16, :] = xs[slot, h, r + 1, 32 * m + 8:32 * m + 24, :] + inc[16 * m:16 * m + 16, h * 128:h * 128 + 128]
             for col in range(columns):
-                for h in range(2):
-                    sb[out_slot, r, col, :, h * 128:h * 128 + 128] = ts[h, pl.ds(col, members, stride=16), :].astype(jnp.bfloat16)
+                sb1[out_slot, r, col] = ts[0, pl.ds(col, members, stride=16), :].astype(jnp.bfloat16)
+                t2[r, col] = ts[1, pl.ds(col, members, stride=16), :]
             return carry
         lax.fori_loop(0, 4, block, 0)
 
         @pl.when(dslot < 3)
         def _():
-            unit_copy(patch, dslot).start()
+            def pack(pair, carry):
+                left = jnp.zeros((members, 128), jnp.float32)
+                for k in range(8):
+                    r, c0 = pair * 2 + k // 4, (k % 4) * 4
+                    v = [t2[r, c0 + i] for i in range(4)]
+                    for i in range(3):
+                        sb2[out_slot, pair * 25 + k * 3 + i] = jnp.where(lane < 96, v[i], pltpu.roll(v[3], 96 - 32 * i, 1)).astype(jnp.bfloat16)
+                    for i in range(4):
+                        left = left + pltpu.roll(jnp.where(lane >= 96, v[i], 0.0), (32 + 3 * (4 * k + i)) % 128, 1)
+                sb2[out_slot, pair * 25 + 24] = left.astype(jnp.bfloat16)
+                return carry
+            lax.fori_loop(0, 2, pack, 0)
+            for copy in unit_copies(patch, dslot):
+                copy.start()
 
         @pl.when(dslot == 3)
         def _():
             def own(r, carry):
-                gath[patch, r, :, pl.ds(pl.multiple_of(me * members, members), members), :] = sb[patches * 3, r]
+                for col in range(columns):
+                    gath[patch, r, col, mine, 0:128] = sb1[patches * 3, r, col]
+                    gath[patch, r, col, mine, 128:256] = t2[r, col].astype(jnp.bfloat16)
                 return carry
             lax.fori_loop(0, 4, own, 0)
 
+    def unpack(patch, dslot):
+        src = pl.ds(pl.multiple_of(dest_of(dslot) * members, members), members)
+        box = patch * 3 + dslot
+
+        def half(pair, carry):
+            left = rb[box, pair * 25 + 24].astype(jnp.float32)
+            for k in range(8):
+                r, c0 = pair * 2 + k // 4, (k % 4) * 4
+                p = [rb[box, pair * 25 + k * 3 + i].astype(jnp.float32) for i in range(3)]
+                tail = [jnp.where(lane < 99, pltpu.roll(left, (96 - 3 * (4 * k + i)) % 128, 1), 0.0) for i in range(4)]
+                for i in range(3):
+                    gath[patch, r, c0 + i, src, 128:256] = jnp.where(lane < 96, p[i], tail[i]).astype(jnp.bfloat16)
+                last = jnp.where(lane < 64, jnp.where(lane < 32, pltpu.roll(p[0], 32, 1), pltpu.roll(p[1], 64, 1)),
+                                 jnp.where(lane < 96, pltpu.roll(p[2], 96, 1), tail[3]))
+                gath[patch, r, c0 + 3, src, 128:256] = last.astype(jnp.bfloat16)
+            return carry
+        lax.fori_loop(0, 2, half, 0)
+
     def analysis(patch):
-        for dslot in range(3):
-            unit_copy(patch, dslot).wait_recv()
+        def arrive(dslot, carry):
+            for copy in unit_copies(patch, dslot):
+                copy.wait_recv()
+            unpack(patch, dslot)
+            return carry
+        lax.fori_loop(0, 3, lambda i, c: arrive(2 - i, c), 0)
         gath_copy(patch).start()
         eye = (lax.broadcasted_iota(jnp.int32, (total_m, total_m), 0) == lax.broadcasted_iota(jnp.int32, (total_m, total_m), 1)).astype(jnp.float32)
         csum = jnp.zeros((total_m, CP), jnp.float32)
@@ -174,8 +251,8 @@
                 y = yb[r * total_m:(r + 1) * total_m]
                 ybar = jnp.sum(y, axis=0, keepdims=True) * (1.0 / total_m)
                 y = y - ybar
-                c = y * wt_ref[patch, g:g + 1, :]
-                csum = csum + c * (yo_ref[patch, g:g + 1, :] - ybar)
+                c = y * obs_row[1, patch, g:g + 1, :]
+                csum = csum + c * (obs_row[0, patch, g:g + 1, :] - ybar)
                 yp[g] = y
                 cm[g] = c
         a_mat = (total_m - 1.0) * eye
@@ -204,6 +281,10 @@
         def _():
             forecast(v - 1)
 
+        @pl.when(v == 3)
+        def _():
+            setup()
+
         @pl.when((v >= 12) & (v % 4 == 0))
         def _():
             analysis(v // 4 - 3)
@@ -212,7 +293,8 @@
 
     def finish(patch, carry):
         for dslot in range(3):
-            unit_copy(patch, dslot).wait_send()
+            for copy in unit_copies(patch, dslot):
+                copy.wait_send()
         for dslot in range(4):
             ghost_copy(patch * 4 + dslot).wait_send()
         gath_copy(patch).wait()
@@ -221,16 +303,16 @@
 
 
 def update_kernel(tt_ref, g_ref, out_ref):
-    t = tt_ref[0]
-    hi = t.astype(jnp.bfloat16)
-    r1 = t - hi.astype(jnp.float32)
-    mid = r1.astype(jnp.bfloat16)
-    low = (r1 - mid.astype(jnp.float32)).astype(jnp.bfloat16)
-    lhs = jnp.concatenate([hi, mid, low], axis=0)
-    n = t.shape[0]
+    hi, mid, low = split3(tt_ref[0])
+    n = tt_ref.shape[1]
+    zero = jnp.zeros((n, n), jnp.float32)
+    lhs = jnp.concatenate([
+        jnp.concatenate([hi.astype(jnp.float32), mid.astype(jnp.float32)], axis=1),
+        jnp.concatenate([low.astype(jnp.float32), zero], axis=1)], axis=0).astype(jnp.bfloat16)
     for col in range(g_ref.shape[2]):
-        res = jnp.dot(lhs, g_ref[0, 0, col], preferred_element_type=jnp.float32)
-        val = (res[2 * n:] + res[n:2 * n]) + res[:n]
+        g = g_ref[0, 0, col]
+        res = jnp.dot(lhs, jnp.concatenate([g, g], axis=0), preferred_element_type=jnp.float32)
+        val = res[n:] + res[:n]
         out_ref[0, col] = val[:, :out_ref.shape[3]].astype(jnp.bfloat16)
 
 
@@ -240,23 +322,10 @@
 
     def local_step(ens_state, w_in, w_out, obs_op, obs_val, obs_wt):
         members, rows, columns, channels = ens_state.shape
-        hidden = w_in.shape[1]
         total_m = members * ens_size
         dev_rows = rows // ens_size
         patches = dev_rows // 4
         units = patches * ens_size
-        obs = obs_op.shape[1]
-        pad = ((0, CP - channels), (0, 0))
-        wi = jnp.concatenate([jnp.pad(w_in[:channels], pad), jnp.pad(w_in[channels:], pad)], axis=0)
-        wo = jnp.pad(w_out, ((0, 0), (0, CP - channels)))
-        op = jnp.pad(obs_op, pad)
-        start = lax.axis_index("ens") * patches
-
-        def arrange(v):
-            v = lax.dynamic_slice_in_dim(v, start, patches, axis=0)
-            v = v.reshape(patches, 4, 2, 8 * obs).transpose(0, 2, 1, 3)
-            return v.reshape(patches, 8, 8 * obs)
-        yo, wt = arrange(obs_val), arrange(obs_wt)
         dims = (members, rows, columns, channels, patches, dev_rows, ens_size)
         vmem = pl.BlockSpec(memory_space=pltpu.VMEM)
         anym = pl.BlockSpec(memory_space=pl.ANY)
@@ -266,24 +335,32 @@
             functools.partial(exchange_kernel, dims),
             out_shape=(jax.ShapeDtypeStruct((patches, 4, columns, total_m, CP), bf),
                        jax.ShapeDtypeStruct((patches, total_m, total_m), f32)),
-            in_specs=[anym, vmem, vmem, vmem, vmem, vmem],
+            in_specs=[anym, vmem, vmem, vmem, anym, anym],
             out_specs=(anym, vmem),
             scratch_shapes=[
                 pltpu.VMEM((2, members, 6, columns, channels), bf),
                 pltpu.VMEM((2, 2, 6, members * 32, 128), f32),
                 pltpu.VMEM((members * columns, 2 * CP), bf),
                 pltpu.VMEM((2, members * columns, 128), f32),
-                pltpu.VMEM((patches * 3 + 1, 4, columns, members, CP), bf),
+                pltpu.VMEM((4, columns, members, 128), f32),
+                pltpu.VMEM((patches * 3 + 1, 4, columns, members, 128), bf),
+                pltpu.VMEM((patches * 3, 50, members, 128), bf),
+                pltpu.VMEM((patches * 3, 50, members, 128), bf),
                 pltpu.VMEM((patches, 4, columns, total_m, CP), bf),
                 pltpu.VMEM((units, 2, 4, members, CP), bf),
                 pltpu.VMEM((units, 2, 4, members, CP), bf),
+                pltpu.VMEM((2 * CP, 512), bf),
+                pltpu.VMEM((512, CP), bf),
+                pltpu.VMEM((488, 512), f32),
                 pltpu.VMEM((8 * CP, CP), bf),
+                pltpu.VMEM((2, patches, 4, 1, columns, 32), f32),
+                pltpu.VMEM((2, patches, 8, CP), f32),
                 pltpu.VMEM((8, total_m, CP), f32),
                 pltpu.VMEM((8, total_m, CP), f32),
-                dma((2, 3)), dma((units,)), dma((units,)), dma((patches, 3)), dma((patches, 3)), dma((patches,)),
+                dma((2, 3)), dma((units,)), dma((units,)), dma((patches, 3, 2)), dma((patches, 3, 2)), dma((patches,)), dma((2,)),
             ],
             compiler_params=pltpu.CompilerParams(collective_id=0, has_side_effects=True, vmem_limit_bytes=62 * 1024 * 1024),
-        )(ens_state, wi, wo, op, yo, wt)
+        )(ens_state, w_in, w_out.T, obs_op.T, obs_val, obs_wt)
         return pl.pallas_call(
             update_kernel,
             grid=(patches, 4),

time: 268 us -> 246 us (0.918)
  the two profiles are of different devices: /device:TPU:1 before, /device:TPU:0 now
where the time goes in v2:
time: 246 us; the launch traced here: 244 us
  Pallas kernels  219 us (89%)
  local copies, waits for them, and re-layouts  24.8 us (10%)
    pallas_call x1, Pallas kernels, local_step(): pl.pallas_call(functools.partial(exchange_kernel, dims), out_shape=(jax.S...  190 us
    pallas_call x1, Pallas kernels, local_step(): pl.pallas_call(update_kernel, grid=(patches, 4), out_shape=jax.ShapeDtype...  29.3 us
    unnamed x1, local copies, waits for them, and re-layouts  24.8 us

profile of v2, /device:TPU:0, one launch (start us, length us, event | category | flops | bytes accessed | tf_op | source)
XLA Modules:
  0.0 244.3 jit_solution(10339132113945929276)
XLA Ops:
  0.0 24.8 %copy.7.x_hbm = bf16[16,128,16,227]{3,2,1,0:T(8,128)(2,1)} copy(bf16[16,128,16,227]{1,2,3,0:T(8,128)(2,1)} %param.6) | data formatting | bytes 29753344 | tf_op args[0]
  24.8 190.2 %shard_map.64 = (bf16[8,4,16,64,256]{4,3,2,1,0:T(8,128)(2,1)}, f32[8,64,64]{2,1,0:T(8,128)}) custom-call(bf16[16,128,16,227]{3,2,1,0:T(8,128)(2,1)} %copy.7.x_hbm, bf16[454,512]{1,0:T(8,128)(2,1)} %wi_ref.1, bf16[227,512]{1,0:T(8,128)(2,1)} %bitcast.2, bf16[32,227]{1,0:T(8,128)(2,1)} %bitcast.3, f32[32,4,1,16,32]{4,3,2,1,0:T(8,128)} %yo_hbm.1, ...), custom_call_target="tpu_custom_call" | custom-call | tf_op jit(solution)/shard_map/pallas_call | solution.py:334
  215.0 29.3 %shard_map.65 = bf16[32,16,64,227]{3,2,1,0:T(8,128)(2,1)} custom-call(f32[8,64,64]{2,1,0:T(8,128)} %get-tuple-element.7.tt_ref, bf16[8,4,16,64,256]{4,3,2,1,0:T(8,128)(2,1)} %get-tuple-element.8.g_ref), custom_call_target="tpu_custom_call" | custom-call | tf_op jit(solution)/shard_map/pallas_call | solution.py:364

commit v3 on v2

--- a/solution.py
+++ b/solution.py
@@ -16,6 +16,11 @@
 NN = (((1,), (0,)), ((), ()))
 
 
+def gelu(x):
+    scale = math.sqrt(2.0 / math.pi)
+    return (0.5 * x) * (1.0 + jnp.tanh(x * (scale + (scale * 0.044715) * (x * x))))
+
+
 def split3(a):
     hi = a.astype(jnp.bfloat16)
     rem = a - hi.astype(jnp.float32)
@@ -38,8 +43,28 @@
     return (small + (by_mid[:n] + by_hi[n:2 * n])) + by_hi[:n]
 
 
+def pair_lhs(a):
+    hi, mid, low = split3(a)
+    first = lax.broadcasted_iota(jnp.int32, a.shape, 1) < a.shape[1] // 2
+    hi, mid, low = (v.astype(jnp.float32) for v in (hi, mid, low))
+    lead = jnp.where(first, hi, mid).astype(jnp.bfloat16)
+    return jnp.concatenate([lead, lead, jnp.where(first, hi, low).astype(jnp.bfloat16)], axis=1)
+
+
+def pair_rhs(b):
+    hi, mid, low = split3(b)
+    return jnp.concatenate([hi, hi, mid, mid, low, hi], axis=0)
+
+
+def twin_dot(lhs, rhs):
+    k = rhs.shape[1]
+    acc = jnp.dot(lhs[:, 2*k:], rhs[2*k:], preferred_element_type=jnp.float32)
+    acc = acc + jnp.dot(lhs[:, k:2*k], rhs[k:2*k], preferred_element_type=jnp.float32)
+    return acc + jnp.dot(lhs[:, :k], rhs[:k], preferred_element_type=jnp.float32)
+
+
 def exchange_kernel(dims, x_hbm, wi_ref, wo_ref, op_ref, yo_hbm, wt_hbm, g_hbm, tt_ref,
-                    xv, xs, xl, ts, t2, sb1, sb2, rb, gath, gsend, grecv, wi, wo, wf, wobs, obs_raw, obs_row, yp, cm,
+                    xv, xs, xl, ts, t2, sb1, sb2, rb, gath, gsend, grecv, wi, wo, wf, wobs, obs_raw, obs_row, yp, cm, amat, cvec,
                     xsem, gssem, grsem, ssem, rsem, gsem, osem):
     members, rows, columns, channels, patches, dev_rows, ens_size = dims
     rest = channels - 128
@@ -178,7 +203,7 @@
                     xl[16 * m:16 * m + 16, h * 128:h * 128 + 128] = cur.astype(jnp.bfloat16)
                     xl[16 * m:16 * m + 16, CP + h * 128:CP + h * 128 + 128] = lap.astype(jnp.bfloat16)
             hidden = jnp.dot(xl[...], wi[...], preferred_element_type=jnp.float32)
-            gel = jax.nn.gelu(hidden, approximate=True).astype(jnp.bfloat16)
+            gel = gelu(hidden).astype(jnp.bfloat16)
             inc = jnp.dot(gel, wo[...], preferred_element_type=jnp.float32)
             for m in range(members):
                 for h in range(2):
@@ -258,19 +283,31 @@
         a_mat = (total_m - 1.0) * eye
         for g in range(8):
             a_mat = a_mat + f32dot(cm[g], yp[g], NT)
-        trace = jnp.sum(jnp.sum(a_mat * eye, axis=0, keepdims=True), axis=1, keepdims=True)
+        amat[patch % 2, :, 0:total_m] = a_mat
+        amat[patch % 2, :, total_m:2 * total_m] = a_mat
+        cvec[patch % 2] = jnp.broadcast_to(jnp.sum(csum, axis=1, keepdims=True), (total_m, 2 * total_m))
+
+    def solve(patch):
+        row = lax.broadcasted_iota(jnp.int32, (total_m, 2 * total_m), 0)
+        col = lax.broadcasted_iota(jnp.int32, (total_m, 2 * total_m), 1)
+        eye = ((row == col) | (row + total_m == col)).astype(jnp.float32)
+        mats = [amat[i] for i in range(2)]
+        traces = [0.5 * jnp.sum(jnp.sum(a * eye, axis=0, keepdims=True), axis=1, keepdims=True) for a in mats]
 
         def newton(step, carry):
-            y, z = carry
-            mix = 1.5 * eye - 0.5 * f32dot(z, y)
-            return f32dot(y, mix), f32dot(mix, z)
-        _, inv = lax.fori_loop(0, NS_STEPS, newton, (a_mat / trace, eye))
-        root = inv / jnp.sqrt(trace)
-        rhs = jnp.broadcast_to(jnp.sum(csum, axis=1, keepdims=True), (total_m, total_m))
-        wbar = f32dot(root, f32dot(root, rhs))
-        trans = math.sqrt(total_m - 1.0) * root + wbar
-        trans = trans + (1.0 - jnp.sum(trans, axis=0, keepdims=True)) * (1.0 / total_m)
-        tt_ref[patch] = trans.T
+            out = []
+            for y, z in carry:
+                mix = 1.5 * eye - 0.5 * twin_dot(pair_lhs(z), pair_rhs(y))
+                out.append((twin_dot(pair_lhs(y), pair_rhs(mix)), twin_dot(pair_lhs(mix), pair_rhs(z))))
+            return tuple(out)
+        pairs = lax.fori_loop(0, NS_STEPS, newton, tuple((a / t, eye) for a, t in zip(mats, traces)))
+        for i in range(2):
+            root = pairs[i][1] / jnp.sqrt(traces[i])
+            left = pair_lhs(root)
+            wbar = twin_dot(left, pair_rhs(twin_dot(left, pair_rhs(cvec[i]))))
+            trans = math.sqrt(total_m - 1.0) * root + wbar
+            trans = trans + (1.0 - jnp.sum(trans, axis=0, keepdims=True)) * (1.0 / total_m)
+            tt_ref[patch + i] = trans[:, 0:total_m].T
 
     def step(v, carry):
         @pl.when(v < units)
@@ -288,6 +325,10 @@
         @pl.when((v >= 12) & (v % 4 == 0))
         def _():
             analysis(v // 4 - 3)
+
+        @pl.when((v >= 12) & (v % 8 == 0))
+        def _():
+            solve(v // 4 - 4)
         return carry
     lax.fori_loop(0, units + 9, step, 0)
 
@@ -309,11 +350,15 @@
     lhs = jnp.concatenate([
         jnp.concatenate([hi.astype(jnp.float32), mid.astype(jnp.float32)], axis=1),
         jnp.concatenate([low.astype(jnp.float32), zero], axis=1)], axis=0).astype(jnp.bfloat16)
-    for col in range(g_ref.shape[2]):
-        g = g_ref[0, 0, col]
-        res = jnp.dot(lhs, jnp.concatenate([g, g], axis=0), preferred_element_type=jnp.float32)
-        val = res[n:] + res[:n]
-        out_ref[0, col] = val[:, :out_ref.shape[3]].astype(jnp.bfloat16)
+
+    def row(r, carry):
+        for col in range(g_ref.shape[2]):
+            g = g_ref[0, r, col]
+            res = jnp.dot(lhs, jnp.concatenate([g, g], axis=0), preferred_element_type=jnp.float32)
+            val = res[n:] + res[:n]
+            out_ref[r, col] = val[:, :out_ref.shape[3]].astype(jnp.bfloat16)
+        return carry
+    lax.fori_loop(0, g_ref.shape[1], row, 0)
 
 
 def solution(mesh):
@@ -357,18 +402,20 @@
                 pltpu.VMEM((2, patches, 8, CP), f32),
                 pltpu.VMEM((8, total_m, CP), f32),
                 pltpu.VMEM((8, total_m, CP), f32),
+                pltpu.VMEM((2, total_m, 2 * total_m), f32),
+                pltpu.VMEM((2, total_m, 2 * total_m), f32),
                 dma((2, 3)), dma((units,)), dma((units,)), dma((patches, 3, 2)), dma((patches, 3, 2)), dma((patches,)), dma((2,)),
             ],
             compiler_params=pltpu.CompilerParams(collective_id=0, has_side_effects=True, vmem_limit_bytes=62 * 1024 * 1024),
         )(ens_state, w_in, w_out.T, obs_op.T, obs_val, obs_wt)
         return pl.pallas_call(
             update_kernel,
-            grid=(patches, 4),
+            grid=(patches,),
             out_shape=jax.ShapeDtypeStruct((dev_rows, columns, total_m, channels), bf),
-            in_specs=[pl.BlockSpec((1, total_m, total_m), lambda p, r: (p, 0, 0)),
-                      pl.BlockSpec((1, 1, columns, total_m, CP), lambda p, r: (p, r, 0, 0, 0))],
-            out_specs=pl.BlockSpec((1, columns, total_m, channels), lambda p, r: (p * 4 + r, 0, 0, 0)),
-            compiler_params=pltpu.CompilerParams(dimension_semantics=("arbitrary", "arbitrary")),
+            in_specs=[pl.BlockSpec((1, total_m, total_m), lambda p: (p, 0, 0)),
+                      pl.BlockSpec((1, 4, columns, total_m, CP), lambda p: (p, 0, 0, 0, 0))],
+            out_specs=pl.BlockSpec((4, columns, total_m, channels), lambda p: (p, 0, 0, 0)),
+            compiler_params=pltpu.CompilerParams(dimension_semantics=("arbitrary",)),
         )(trans, gathered)
 
     return jax.shard_map(local_step, mesh=mesh, in_specs=(P("ens", None, "dom", None), P(), P(), P(), obs_spec, obs_spec), out_specs=P("ens", "dom", None, None), check_vma=False)

time: 246 us -> 232 us (0.943)
  the two profiles are of different devices: /device:TPU:0 before, /device:TPU:1 now
where the time goes in v3:
time: 232 us; the launch traced here: 231 us
  Pallas kernels  206 us (89%)
  local copies, waits for them, and re-layouts  24.8 us (11%)
    pallas_call x1, Pallas kernels, local_step(): pl.pallas_call(functools.partial(exchange_kernel, dims), out_shape=(jax.S...  187 us
    unnamed x1, local copies, waits for them, and re-layouts  24.8 us
    pallas_call x1, Pallas kernels, local_step(): pl.pallas_call(update_kernel, grid=(patches,), out_shape=jax.ShapeDtypeSt...  19.3 us

profile of v3, /device:TPU:1, one launch (start us, length us, event | category | flops | bytes accessed | tf_op | source)
XLA Modules:
  0.0 231.0 jit_solution(17200447569214222469)
XLA Ops:
  0.0 24.8 %copy.7.x_hbm = bf16[16,128,16,227]{3,2,1,0:T(8,128)(2,1)} copy(bf16[16,128,16,227]{1,2,3,0:T(8,128)(2,1)} %param.6) | data formatting | bytes 29753344 | tf_op args[0]
  24.8 186.9 %shard_map.64 = (bf16[8,4,16,64,256]{4,3,2,1,0:T(8,128)(2,1)}, f32[8,64,64]{2,1,0:T(8,128)}) custom-call(bf16[16,128,16,227]{3,2,1,0:T(8,128)(2,1)} %copy.7.x_hbm, bf16[454,512]{1,0:T(8,128)(2,1)} %wi_ref.1, bf16[227,512]{1,0:T(8,128)(2,1)} %bitcast.2, bf16[32,227]{1,0:T(8,128)(2,1)} %bitcast.3, f32[32,4,1,16,32]{4,3,2,1,0:T(8,128)} %yo_hbm.1, ...), custom_call_target="tpu_custom_call" | custom-call | tf_op jit(solution)/shard_map/pallas_call | solution.py:379
  211.7 19.3 %shard_map.65 = bf16[32,16,64,227]{3,2,1,0:T(8,128)(2,1)} custom-call(f32[8,64,64]{2,1,0:T(8,128)} %get-tuple-element.7.tt_ref, bf16[8,4,16,64,256]{4,3,2,1,0:T(8,128)(2,1)} %get-tuple-element.8.g_ref), custom_call_target="tpu_custom_call" | custom-call | tf_op jit(solution)/shard_map/pallas_call | solution.py:411

commit v4 on v3

--- a/solution.py
+++ b/solution.py
@@ -63,11 +63,10 @@
     return acc + jnp.dot(lhs[:, :k], rhs[:k], preferred_element_type=jnp.float32)
 
 
-def exchange_kernel(dims, x_hbm, wi_ref, wo_ref, op_ref, yo_hbm, wt_hbm, g_hbm, tt_ref,
-                    xv, xs, xl, ts, t2, sb1, sb2, rb, gath, gsend, grecv, wi, wo, wf, wobs, obs_raw, obs_row, yp, cm, amat, cvec,
+def exchange_kernel(dims, xt_hbm, wi_ref, wo_ref, op_ref, yo_hbm, wt_hbm, g_hbm, tt_ref,
+                    xn, xb, xs, xl, ts, t2, sb1, sb2, rb, gath, gsend, grecv, wi, wo, wf, wobs, obs_raw, obs_row, yp, cm, amat, cvec,
                     xsem, gssem, grsem, ssem, rsem, gsem, osem):
     members, rows, columns, channels, patches, dev_rows, ens_size = dims
-    rest = channels - 128
     units = patches * ens_size
     total_m = members * ens_size
     me = lax.axis_index("ens")
@@ -80,15 +79,8 @@
         dc = (my_core + (dslot + 1) // 2) % 2
         return dx * 2 + dc
 
-    def x_copies(unit, action):
-        patch, dslot = unit // ens_size, unit % ens_size
-        slot = unit % 2
-        first = dest_of(dslot) * dev_rows + patch * 4
-        north = jnp.maximum(first - 1, 0)
-        south = jnp.minimum(first + 4, rows - 1)
-        for idx, (src, num, dst) in enumerate(((first, 4, 1), (north, 1, 0), (south, 1, 5))):
-            copy = pltpu.make_async_copy(x_hbm.at[:, pl.ds(src, num)], xv.at[slot, :, pl.ds(dst, num)], xsem.at[slot, idx])
-            action(copy)
+    def x_copy(m):
+        return pltpu.make_async_copy(xt_hbm.at[m], xn.at[m % 2], xsem.at[m % 2])
 
     def ghost_copy(unit):
         return pltpu.make_async_remote_copy(
@@ -98,11 +90,11 @@
     def unit_copies(patch, dslot):
         dev = {"ens": dest_of(dslot)}
         first = pltpu.make_async_remote_copy(
-            src_ref=sb1.at[patch * 3 + dslot], dst_ref=gath.at[patch, :, :, mine, pl.ds(0, 128)],
+            src_ref=sb1.at[(patch % 3) * 3 + dslot], dst_ref=gath.at[patch, :, :, mine, pl.ds(0, 128)],
             send_sem=ssem.at[patch, dslot, 0], recv_sem=rsem.at[patch, dslot, 0],
             device_id=dev, device_id_type=MESH)
         second = pltpu.make_async_remote_copy(
-            src_ref=sb2.at[patch * 3 + dslot], dst_ref=rb.at[patch * 3 + dslot],
+            src_ref=sb2.at[(patch % 3) * 3 + dslot], dst_ref=rb.at[patch * 3 + dslot],
             send_sem=ssem.at[patch, dslot, 1], recv_sem=rsem.at[patch, dslot, 1],
             device_id=dev, device_id_type=MESH)
         return first, second
@@ -112,7 +104,7 @@
 
     obs_copies = [pltpu.make_async_copy(ref.at[pl.ds(me * patches, patches)], obs_raw.at[i], osem.at[i]) for i, ref in enumerate((yo_hbm, wt_hbm))]
 
-    x_copies(0, lambda c: c.start())
+    x_copy(0).start()
     for copy in obs_copies:
         copy.start()
     barrier = pltpu.get_barrier_semaphore()
@@ -120,7 +112,7 @@
         pl.semaphore_signal(barrier, inc=1, device_id={"ens": dest_of(dslot)}, device_id_type=MESH)
     pl.semaphore_signal(barrier, inc=1, device_id={"dom": 1 - mydom}, device_id_type=MESH)
 
-    xs[:, 1] = jnp.zeros((2, 6, members * 32, 128), jnp.float32)
+    xs[0, 1, 3, 16 * (channels % 32):512, :] = jnp.zeros((512 - 16 * (channels % 32), 128), jnp.float32)
     wf[...] = jnp.zeros_like(wf)
     wf[0:channels, :] = wo_ref[...].astype(jnp.float32)
     wo[...] = wf[0:CP, :].T.astype(jnp.bfloat16)
@@ -128,6 +120,36 @@
     keep = lax.broadcasted_iota(jnp.int32, (CP, 512), 0) < channels
     wi[0:CP, :] = jnp.where(keep, wf[0:CP, :], 0.0).astype(jnp.bfloat16)
     wi[CP:2 * CP, :] = wf[channels:channels + CP, :].astype(jnp.bfloat16)
+    turn = (lax.broadcasted_iota(jnp.int32, (128, 128), 0) == lax.broadcasted_iota(jnp.int32, (128, 128), 1)).astype(jnp.float32).astype(jnp.bfloat16)
+
+    def relayout(m, carry):
+        @pl.when(m + 1 < members)
+        def _():
+            x_copy(m + 1).start()
+        x_copy(m).wait()
+
+        def widen(b, c2):
+            for cc in range(32):
+                xs[0, b // 4, b % 4, 16 * cc:16 * cc + 16, :] = xn[m % 2, b * 32 + cc].astype(jnp.float32)
+            return c2
+        lax.fori_loop(0, channels // 32, widen, 0)
+        for cc in range(channels % 32):
+            xs[0, 1, 3, 16 * cc:16 * cc + 16, :] = xn[m % 2, channels - channels % 32 + cc].astype(jnp.float32)
+        for col in range(columns):
+            part = jnp.concatenate([xs[0, h, j, pl.ds(col, 32, stride=16), :] for h in range(2) for j in range(4)], axis=0)
+            out = lax.dot_general(turn, part.astype(jnp.bfloat16), NT, preferred_element_type=jnp.float32)
+            for h in range(2):
+                for j in range(4):
+                    xs[1, h, j, pl.ds(col, 32, stride=16), :] = out[32 * j:32 * j + 32, h * 128:h * 128 + 128]
+
+        def narrow(j, c2):
+            for rr in range(32):
+                for h in range(2):
+                    xb[m, 32 * j + rr, :, h * 128:h * 128 + 128] = xs[1, h, j, 16 * rr:16 * rr + 16, :].astype(jnp.bfloat16)
+            return c2
+        lax.fori_loop(0, 4, narrow, 0)
+        return carry
+    lax.fori_loop(0, members, relayout, 0)
     pl.semaphore_wait(barrier, 4)
 
     lane = lax.broadcasted_iota(jnp.int32, (members, 128), 1)
@@ -159,17 +181,14 @@
 
     def prepare(unit):
         slot = unit % 2
-
-        @pl.when(unit + 1 < units)
-        def _():
-            x_copies(unit + 1, lambda c: c.start())
-        x_copies(unit, lambda c: c.wait())
+        patch, dslot = unit // ens_size, unit % ens_size
+        first = dest_of(dslot) * dev_rows + patch * 4
 
         def convert(r, carry):
+            row = jnp.minimum(jnp.maximum(first + r - 1, 0), rows - 1)
             for m in range(members):
-                v = xv[slot, m, r]
-                xs[slot, 0, r, 32 * m + 8:32 * m + 24, :] = v[:, :128].astype(jnp.float32)
-                xs[slot, 1, r, 32 * m + 8:32 * m + 24, 0:rest] = v[:, 128:].astype(jnp.float32)
+                for h in range(2):
+                    xs[slot, h, r, 32 * m + 8:32 * m + 24, :] = xb[m, row, :, h * 128:h * 128 + 128].astype(jnp.float32)
             return carry
         lax.fori_loop(0, 6, convert, 0)
 
@@ -184,7 +203,12 @@
     def forecast(unit):
         patch, dslot = unit // ens_size, unit % ens_size
         slot = unit % 2
-        out_slot = jnp.where(dslot < 3, patch * 3 + dslot, patches * 3)
+        out_slot = jnp.where(dslot < 3, (patch % 3) * 3 + dslot, 9)
+
+        @pl.when((dslot < 3) & (patch >= 3))
+        def _():
+            for copy in unit_copies(patch - 3, dslot):
+                copy.wait_send()
         ghost_copy(unit).wait_recv()
 
         def block(r, carry):
@@ -235,7 +259,7 @@
         def _():
             def own(r, carry):
                 for col in range(columns):
-                    gath[patch, r, col, mine, 0:128] = sb1[patches * 3, r, col]
+                    gath[patch, r, col, mine, 0:128] = sb1[9, r, col]
                     gath[patch, r, col, mine, 128:256] = t2[r, col].astype(jnp.bfloat16)
                 return carry
             lax.fori_loop(0, 4, own, 0)
@@ -333,9 +357,11 @@
     lax.fori_loop(0, units + 9, step, 0)
 
     def finish(patch, carry):
-        for dslot in range(3):
-            for copy in unit_copies(patch, dslot):
-                copy.wait_send()
+        @pl.when(patch >= patches - 3)
+        def _():
+            for dslot in range(3):
+                for copy in unit_copies(patch, dslot):
+                    copy.wait_send()
         for dslot in range(4):
             ghost_copy(patch * 4 + dslot).wait_send()
         gath_copy(patch).wait()
@@ -383,13 +409,14 @@
             in_specs=[anym, vmem, vmem, vmem, anym, anym],
             out_specs=(anym, vmem),
             scratch_shapes=[
-                pltpu.VMEM((2, members, 6, columns, channels), bf),
+                pltpu.VMEM((2, channels, columns, rows), bf),
+                pltpu.VMEM((members, rows, columns, CP), bf),
                 pltpu.VMEM((2, 2, 6, members * 32, 128), f32),
                 pltpu.VMEM((members * columns, 2 * CP), bf),
                 pltpu.VMEM((2, members * columns, 128), f32),
                 pltpu.VMEM((4, columns, members, 128), f32),
-                pltpu.VMEM((patches * 3 + 1, 4, columns, members, 128), bf),
-                pltpu.VMEM((patches * 3, 50, members, 128), bf),
+                pltpu.VMEM((10, 4, columns, members, 128), bf),
+                pltpu.VMEM((9, 50, members, 128), bf),
                 pltpu.VMEM((patches * 3, 50, members, 128), bf),
                 pltpu.VMEM((patches, 4, columns, total_m, CP), bf),
                 pltpu.VMEM((units, 2, 4, members, CP), bf),
@@ -404,10 +431,10 @@
                 pltpu.VMEM((8, total_m, CP), f32),
                 pltpu.VMEM((2, total_m, 2 * total_m), f32),
                 pltpu.VMEM((2, total_m, 2 * total_m), f32),
-                dma((2, 3)), dma((units,)), dma((units,)), dma((patches, 3, 2)), dma((patches, 3, 2)), dma((patches,)), dma((2,)),
+                dma((2,)), dma((units,)), dma((units,)), dma((patches, 3, 2)), dma((patches, 3, 2)), dma((patches,)), dma((2,)),
             ],
             compiler_params=pltpu.CompilerParams(collective_id=0, has_side_effects=True, vmem_limit_bytes=62 * 1024 * 1024),
-        )(ens_state, w_in, w_out.T, obs_op.T, obs_val, obs_wt)
+        )(ens_state.transpose(0, 3, 2, 1), w_in, w_out.T, obs_op.T, obs_val, obs_wt)
         return pl.pallas_call(
             update_kernel,
             grid=(patches,),

time: 232 us -> 234 us (level)
  Pallas kernels: 206 us -> 234 us
  local copies, waits for them, and re-layouts: 24.8 us -> 0 us
    pallas_call x1, Pallas kernels: 187 us -> 215 us  [local_step(): pl.pallas_call(functools.partial(exchange_kernel, dims), out_shape=(jax.S...]
    unnamed x1 -> x0, local copies, waits for them, and re-layouts: 24.8 us -> none
where the time goes in v4:
time: 234 us
  Pallas kernels  234 us (100%)
    pallas_call x1, Pallas kernels, local_step(): pl.pallas_call(functools.partial(exchange_kernel, dims), out_shape=(jax.S...  215 us
    pallas_call x1, Pallas kernels, local_step(): pl.pallas_call(update_kernel, grid=(patches,), out_shape=jax.ShapeDtypeSt...  19.3 us

profile of v4, /device:TPU:1, one launch (start us, length us, event | category | flops | bytes accessed | tf_op | source)
XLA Modules:
  0.0 234.0 jit_solution(3902227627744503510)
XLA Ops:
  0.0 214.7 %shard_map.64 = (bf16[8,4,16,64,256]{4,3,2,1,0:T(8,128)(2,1)}, f32[8,64,64]{2,1,0:T(8,128)}) custom-call(bf16[16,227,16,128]{3,2,1,0:T(8,128)(2,1)} %bitcast.3, bf16[454,512]{1,0:T(8,128)(2,1)} %wi_ref.1, bf16[227,512]{1,0:T(8,128)(2,1)} %bitcast.4, bf16[32,227]{1,0:T(8,128)(2,1)} %bitcast.5, f32[32,4,1,16,32]{4,3,2,1,0:T(8,128)} %yo_hbm.1, ...), custom_call_target="tpu_custom_call" | custom-call | tf_op jit(solution)/shard_map/pallas_call | solution.py:405
  214.7 19.3 %shard_map.65 = bf16[32,16,64,227]{3,2,1,0:T(8,128)(2,1)} custom-call(f32[8,64,64]{2,1,0:T(8,128)} %get-tuple-element.7.tt_ref, bf16[8,4,16,64,256]{4,3,2,1,0:T(8,128)(2,1)} %get-tuple-element.8.g_ref), custom_call_target="tpu_custom_call" | custom-call | tf_op jit(solution)/shard_map/pallas_call | solution.py:438

commit v5 on v4

--- a/solution.py
+++ b/solution.py
@@ -112,7 +112,7 @@
         pl.semaphore_signal(barrier, inc=1, device_id={"ens": dest_of(dslot)}, device_id_type=MESH)
     pl.semaphore_signal(barrier, inc=1, device_id={"dom": 1 - mydom}, device_id_type=MESH)
 
-    xs[0, 1, 3, 16 * (channels % 32):512, :] = jnp.zeros((512 - 16 * (channels % 32), 128), jnp.float32)
+    xs[0, 1, 3, 17 * (channels % 32):544, :] = jnp.zeros((544 - 17 * (channels % 32), 128), jnp.float32)
     wf[...] = jnp.zeros_like(wf)
     wf[0:channels, :] = wo_ref[...].astype(jnp.float32)
     wo[...] = wf[0:CP, :].T.astype(jnp.bfloat16)
@@ -130,22 +130,22 @@
 
         def widen(b, c2):
             for cc in range(32):
-                xs[0, b // 4, b % 4, 16 * cc:16 * cc + 16, :] = xn[m % 2, b * 32 + cc].astype(jnp.float32)
+                xs[0, b // 4, b % 4, 17 * cc:17 * cc + 16, :] = xn[m % 2, b * 32 + cc].astype(jnp.float32)
             return c2
         lax.fori_loop(0, channels // 32, widen, 0)
         for cc in range(channels % 32):
-            xs[0, 1, 3, 16 * cc:16 * cc + 16, :] = xn[m % 2, channels - channels % 32 + cc].astype(jnp.float32)
+            xs[0, 1, 3, 17 * cc:17 * cc + 16, :] = xn[m % 2, channels - channels % 32 + cc].astype(jnp.float32)
         for col in range(columns):
-            part = jnp.concatenate([xs[0, h, j, pl.ds(col, 32, stride=16), :] for h in range(2) for j in range(4)], axis=0)
+            part = jnp.concatenate([xs[0, h, j, pl.ds(col, 32, stride=17), :] for h in range(2) for j in range(4)], axis=0)
             out = lax.dot_general(turn, part.astype(jnp.bfloat16), NT, preferred_element_type=jnp.float32)
             for h in range(2):
                 for j in range(4):
-                    xs[1, h, j, pl.ds(col, 32, stride=16), :] = out[32 * j:32 * j + 32, h * 128:h * 128 + 128]
+                    xs[1, h, j, pl.ds(col, 32, stride=17), :] = out[32 * j:32 * j + 32, h * 128:h * 128 + 128]
 
         def narrow(j, c2):
             for rr in range(32):
                 for h in range(2):
-                    xb[m, 32 * j + rr, :, h * 128:h * 128 + 128] = xs[1, h, j, 16 * rr:16 * rr + 16, :].astype(jnp.bfloat16)
+                    xb[m, 32 * j + rr, :, h * 128:h * 128 + 128] = xs[1, h, j, 17 * rr:17 * rr + 16, :].astype(jnp.bfloat16)
             return c2
         lax.fori_loop(0, 4, narrow, 0)
         return carry
@@ -188,14 +188,14 @@
             row = jnp.minimum(jnp.maximum(first + r - 1, 0), rows - 1)
             for m in range(members):
                 for h in range(2):
-                    xs[slot, h, r, 32 * m + 8:32 * m + 24, :] = xb[m, row, :, h * 128:h * 128 + 128].astype(jnp.float32)
+                    xs[slot, h, r, 33 * m + 8:33 * m + 24, :] = xb[m, row, :, h * 128:h * 128 + 128].astype(jnp.float32)
             return carry
         lax.fori_loop(0, 6, convert, 0)
 
         def edges(r, carry):
             for h in range(2):
-                gsend[unit, 0, r, :, h * 128:h * 128 + 128] = xs[slot, h, r + 1, pl.ds(23, members, stride=32), :].astype(jnp.bfloat16)
-                gsend[unit, 1, r, :, h * 128:h * 128 + 128] = xs[slot, h, r + 1, pl.ds(8, members, stride=32), :].astype(jnp.bfloat16)
+                gsend[unit, 0, r, :, h * 128:h * 128 + 128] = xs[slot, h, r + 1, pl.ds(23, members, stride=33), :].astype(jnp.bfloat16)
+                gsend[unit, 1, r, :, h * 128:h * 128 + 128] = xs[slot, h, r + 1, pl.ds(8, members, stride=33), :].astype(jnp.bfloat16)
             return carry
         lax.fori_loop(0, 4, edges, 0)
         ghost_copy(unit).start()
@@ -213,10 +213,10 @@
 
         def block(r, carry):
             for h in range(2):
-                xs[slot, h, r + 1, pl.ds(7, members, stride=32), :] = grecv[unit, 0, r, :, h * 128:h * 128 + 128].astype(jnp.float32)
-                xs[slot, h, r + 1, pl.ds(24, members, stride=32), :] = grecv[unit, 1, r, :, h * 128:h * 128 + 128].astype(jnp.float32)
+                xs[slot, h, r + 1, pl.ds(7, members, stride=33), :] = grecv[unit, 0, r, :, h * 128:h * 128 + 128].astype(jnp.float32)
+                xs[slot, h, r + 1, pl.ds(24, members, stride=33), :] = grecv[unit, 1, r, :, h * 128:h * 128 + 128].astype(jnp.float32)
             for m in range(members):
-                b = 32 * m
+                b = 33 * m
                 for h in range(2):
                     cur = xs[slot, h, r + 1, b + 8:b + 24, :]
                     north = xs[slot, h, r, b + 8:b + 24, :]
@@ -231,10 +231,10 @@
             inc = jnp.dot(gel, wo[...], preferred_element_type=jnp.float32)
             for m in range(members):
                 for h in range(2):
-                    ts[h, 16 * m:16 * m + 16, :] = xs[slot, h, r + 1, 32 * m + 8:32 * m + 24, :] + inc[16 * m:16 * m + 16, h * 128:h * 128 + 128]
+                    ts[h, 17 * m:17 * m + 16, :] = xs[slot, h, r + 1, 33 * m + 8:33 * m + 24, :] + inc[16 * m:16 * m + 16, h * 128:h * 128 + 128]
             for col in range(columns):
-                sb1[out_slot, r, col] = ts[0, pl.ds(col, members, stride=16), :].astype(jnp.bfloat16)
-                t2[r, col] = ts[1, pl.ds(col, members, stride=16), :]
+                sb1[out_slot, r, col] = ts[0, pl.ds(col, members, stride=17), :].astype(jnp.bfloat16)
+                t2[r, col] = ts[1, pl.ds(col, members, stride=17), :]
             return carry
         lax.fori_loop(0, 4, block, 0)
 
@@ -411,9 +411,9 @@
             scratch_shapes=[
                 pltpu.VMEM((2, channels, columns, rows), bf),
                 pltpu.VMEM((members, rows, columns, CP), bf),
-                pltpu.VMEM((2, 2, 6, members * 32, 128), f32),
+                pltpu.VMEM((2, 2, 6, 544, 128), f32),
                 pltpu.VMEM((members * columns, 2 * CP), bf),
-                pltpu.VMEM((2, members * columns, 128), f32),
+                pltpu.VMEM((2, members * 17, 128), f32),
                 pltpu.VMEM((4, columns, members, 128), f32),
                 pltpu.VMEM((10, 4, columns, members, 128), bf),
                 pltpu.VMEM((9, 50, members, 128), bf),

time: 234 us -> 222 us (0.949)
  Pallas kernels: 234 us -> 222 us
    pallas_call x1, Pallas kernels: 215 us -> 202 us  [local_step(): pl.pallas_call(functools.partial(exchange_kernel, dims), out_shape=(jax.S...]
where the time goes in v5:
time: 222 us
  Pallas kernels  222 us (100%)
    pallas_call x1, Pallas kernels, local_step(): pl.pallas_call(functools.partial(exchange_kernel, dims), out_shape=(jax.S...  202 us
    pallas_call x1, Pallas kernels, local_step(): pl.pallas_call(update_kernel, grid=(patches,), out_shape=jax.ShapeDtypeSt...  19.3 us

profile of v5, /device:TPU:1, one launch (start us, length us, event | category | flops | bytes accessed | tf_op | source)
XLA Modules:
  0.0 221.7 jit_solution(5296371602872195293)
XLA Ops:
  0.0 202.4 %shard_map.64 = (bf16[8,4,16,64,256]{4,3,2,1,0:T(8,128)(2,1)}, f32[8,64,64]{2,1,0:T(8,128)}) custom-call(bf16[16,227,16,128]{3,2,1,0:T(8,128)(2,1)} %bitcast.3, bf16[454,512]{1,0:T(8,128)(2,1)} %wi_ref.1, bf16[227,512]{1,0:T(8,128)(2,1)} %bitcast.4, bf16[32,227]{1,0:T(8,128)(2,1)} %bitcast.5, f32[32,4,1,16,32]{4,3,2,1,0:T(8,128)} %yo_hbm.1, ...), custom_call_target="tpu_custom_call" | custom-call | tf_op jit(solution)/shard_map/pallas_call | solution.py:405
  202.4 19.3 %shard_map.65 = bf16[32,16,64,227]{3,2,1,0:T(8,128)(2,1)} custom-call(f32[8,64,64]{2,1,0:T(8,128)} %get-tuple-element.7.tt_ref, bf16[8,4,16,64,256]{4,3,2,1,0:T(8,128)(2,1)} %get-tuple-element.8.g_ref), custom_call_target="tpu_custom_call" | custom-call | tf_op jit(solution)/shard_map/pallas_call | solution.py:438

commit v6 on v5

--- a/solution.py
+++ b/solution.py
@@ -63,9 +63,9 @@
     return acc + jnp.dot(lhs[:, :k], rhs[:k], preferred_element_type=jnp.float32)
 
 
-def exchange_kernel(dims, xt_hbm, wi_ref, wo_ref, op_ref, yo_hbm, wt_hbm, g_hbm, tt_ref,
-                    xn, xb, xs, xl, ts, t2, sb1, sb2, rb, gath, gsend, grecv, wi, wo, wf, wobs, obs_raw, obs_row, yp, cm, amat, cvec,
-                    xsem, gssem, grsem, ssem, rsem, gsem, osem):
+def exchange_kernel(dims, xt_hbm, wi_ref, wo_ref, op_ref, yo_hbm, wt_hbm, gath, tt_ref,
+                    xn, xb, xs, xl, ts, t2, sb1, sb2, rb, gsend, grecv, wi, wo, wf, wobs, obs_raw, obs_row, yp, cm, amat, cvec,
+                    xsem, gssem, grsem, ssem, rsem, osem):
     members, rows, columns, channels, patches, dev_rows, ens_size = dims
     units = patches * ens_size
     total_m = members * ens_size
@@ -98,9 +98,6 @@
             send_sem=ssem.at[patch, dslot, 1], recv_sem=rsem.at[patch, dslot, 1],
             device_id=dev, device_id_type=MESH)
         return first, second
-
-    def gath_copy(patch):
-        return pltpu.make_async_copy(gath.at[patch], g_hbm.at[patch], gsem.at[patch])
 
     obs_copies = [pltpu.make_async_copy(ref.at[pl.ds(me * patches, patches)], obs_raw.at[i], osem.at[i]) for i, ref in enumerate((yo_hbm, wt_hbm))]
 
@@ -289,7 +286,6 @@
             unpack(patch, dslot)
             return carry
         lax.fori_loop(0, 3, lambda i, c: arrive(2 - i, c), 0)
-        gath_copy(patch).start()
         eye = (lax.broadcasted_iota(jnp.int32, (total_m, total_m), 0) == lax.broadcasted_iota(jnp.int32, (total_m, total_m), 1)).astype(jnp.float32)
         csum = jnp.zeros((total_m, CP), jnp.float32)
         for half in range(2):
@@ -364,13 +360,12 @@
                     copy.wait_send()
         for dslot in range(4):
             ghost_copy(patch * 4 + dslot).wait_send()
-        gath_copy(patch).wait()
         return carry
     lax.fori_loop(0, patches, finish, 0)
 
 
 def update_kernel(tt_ref, g_ref, out_ref):
-    hi, mid, low = split3(tt_ref[0])
+    hi, mid, low = split3(tt_ref[pl.program_id(0)])
     n = tt_ref.shape[1]
     zero = jnp.zeros((n, n), jnp.float32)
     lhs = jnp.concatenate([
@@ -378,13 +373,13 @@
         jnp.concatenate([low.astype(jnp.float32), zero], axis=1)], axis=0).astype(jnp.bfloat16)
 
     def row(r, carry):
-        for col in range(g_ref.shape[2]):
-            g = g_ref[0, r, col]
+        for col in range(out_ref.shape[1]):
+            g = g_ref[pl.program_id(0), r, col]
             res = jnp.dot(lhs, jnp.concatenate([g, g], axis=0), preferred_element_type=jnp.float32)
             val = res[n:] + res[:n]
             out_ref[r, col] = val[:, :out_ref.shape[3]].astype(jnp.bfloat16)
         return carry
-    lax.fori_loop(0, g_ref.shape[1], row, 0)
+    lax.fori_loop(0, out_ref.shape[0], row, 0)
 
 
 def solution(mesh):
@@ -404,10 +399,10 @@
         dma = pltpu.SemaphoreType.DMA
         gathered, trans = pl.pallas_call(
             functools.partial(exchange_kernel, dims),
-            out_shape=(jax.ShapeDtypeStruct((patches, 4, columns, total_m, CP), bf),
-                       jax.ShapeDtypeStruct((patches, total_m, total_m), f32)),
+            out_shape=(pltpu.VMEM((patches, 4, columns, total_m, CP), bf),
+                       pltpu.VMEM((patches, total_m, total_m), f32)),
             in_specs=[anym, vmem, vmem, vmem, anym, anym],
-            out_specs=(anym, vmem),
+            out_specs=(vmem, vmem),
             scratch_shapes=[
                 pltpu.VMEM((2, channels, columns, rows), bf),
                 pltpu.VMEM((members, rows, columns, CP), bf),
@@ -418,7 +413,6 @@
                 pltpu.VMEM((10, 4, columns, members, 128), bf),
                 pltpu.VMEM((9, 50, members, 128), bf),
                 pltpu.VMEM((patches * 3, 50, members, 128), bf),
-                pltpu.VMEM((patches, 4, columns, total_m, CP), bf),
                 pltpu.VMEM((units, 2, 4, members, CP), bf),
                 pltpu.VMEM((units, 2, 4, members, CP), bf),
                 pltpu.VMEM((2 * CP, 512), bf),
@@ -431,18 +425,17 @@
                 pltpu.VMEM((8, total_m, CP), f32),
                 pltpu.VMEM((2, total_m, 2 * total_m), f32),
                 pltpu.VMEM((2, total_m, 2 * total_m), f32),
-                dma((2,)), dma((units,)), dma((units,)), dma((patches, 3, 2)), dma((patches, 3, 2)), dma((patches,)), dma((2,)),
+                dma((2,)), dma((units,)), dma((units,)), dma((patches, 3, 2)), dma((patches, 3, 2)), dma((2,)),
             ],
-            compiler_params=pltpu.CompilerParams(collective_id=0, has_side_effects=True, vmem_limit_bytes=62 * 1024 * 1024),
+            compiler_params=pltpu.CompilerParams(collective_id=0, has_side_effects=True, vmem_limit_bytes=44 * 1024 * 1024),
         )(ens_state.transpose(0, 3, 2, 1), w_in, w_out.T, obs_op.T, obs_val, obs_wt)
         return pl.pallas_call(
             update_kernel,
             grid=(patches,),
             out_shape=jax.ShapeDtypeStruct((dev_rows, columns, total_m, channels), bf),
-            in_specs=[pl.BlockSpec((1, total_m, total_m), lambda p: (p, 0, 0)),
-                      pl.BlockSpec((1, 4, columns, total_m, CP), lambda p: (p, 0, 0, 0, 0))],
+            in_specs=[vmem, vmem],
             out_specs=pl.BlockSpec((4, columns, total_m, channels), lambda p: (p, 0, 0, 0)),
-            compiler_params=pltpu.CompilerParams(dimension_semantics=("arbitrary",)),
-        )(trans, gathered)
+            compiler_params=pltpu.CompilerParams(dimension_semantics=("arbitrary",), vmem_limit_bytes=24 * 1024 * 1024),
+        )(pltpu.with_memory_space_constraint(trans, pltpu.VMEM), pltpu.with_memory_space_constraint(gathered, pltpu.VMEM))
 
     return jax.shard_map(local_step, mesh=mesh, in_specs=(P("ens", None, "dom", None), P(), P(), P(), obs_spec, obs_spec), out_specs=P("ens", "dom", None, None), check_vma=False)

time: 222 us -> 218 us (0.982)
  Pallas kernels: 222 us -> 217 us
    pallas_call x1, Pallas kernels: 19.3 us -> 15.6 us  [local_step(): pl.pallas_call(update_kernel, grid=(patches,), out_shape=jax.ShapeDtypeSt...]
where the time goes in v6:
time: 218 us; the launch traced here: 217 us
  Pallas kernels  217 us (100%)
    pallas_call x1, Pallas kernels, local_step(): pl.pallas_call(functools.partial(exchange_kernel, dims), out_shape=(pltpu...  202 us
    pallas_call x1, Pallas kernels, local_step(): pl.pallas_call(update_kernel, grid=(patches,), out_shape=jax.ShapeDtypeSt...  15.6 us

profile of v6, /device:TPU:1, one launch (start us, length us, event | category | flops | bytes accessed | tf_op | source)
XLA Modules:
  0.0 217.2 jit_solution(15712158632906754880)
XLA Ops:
  0.0 201.6 %shard_map.64 = (bf16[8,4,16,64,256]{4,3,2,1,0:T(8,128)(2,1)S(1)}, f32[8,64,64]{2,1,0:T(8,128)S(1)}) custom-call(bf16[16,227,16,128]{3,2,1,0:T(8,128)(2,1)} %bitcast.3, bf16[454,512]{1,0:T(8,128)(2,1)} %wi_ref.1, bf16[227,512]{1,0:T(8,128)(2,1)} %bitcast.4, bf16[32,227]{1,0:T(8,128)(2,1)} %bitcast.5, f32[32,4,1,16,32]{4,3,2,1,0:T(8,128)} %yo_hbm.1, ...), custom_call_target="tpu_custom_call" | custom-call | tf_op jit(solution)/shard_map/pallas_call | solution.py:400
  201.6 15.6 %shard_map.65 = bf16[32,16,64,227]{3,2,1,0:T(8,128)(2,1)} custom-call(f32[8,64,64]{2,1,0:T(8,128)S(1)} %get-tuple-element.7.tt_ref, bf16[8,4,16,64,256]{4,3,2,1,0:T(8,128)(2,1)S(1)} %get-tuple-element.8.g_ref), custom_call_target="tpu_custom_call" | custom-call | tf_op jit(solution)/shard_map/pallas_call | solution.py:432

commit v7 on v6

--- a/solution.py
+++ b/solution.py
@@ -63,10 +63,23 @@
     return acc + jnp.dot(lhs[:, :k], rhs[:k], preferred_element_type=jnp.float32)
 
 
+def stacked(t):
+    hi, mid, low = (v.astype(jnp.float32) for v in split3(t))
+    return jnp.concatenate([
+        jnp.concatenate([hi, mid], axis=1),
+        jnp.concatenate([low, jnp.zeros_like(low)], axis=1)], axis=0).astype(jnp.bfloat16)
+
+
+def transform(lhs, g):
+    n = lhs.shape[0] // 2
+    res = jnp.dot(lhs, jnp.concatenate([g, g], axis=0), preferred_element_type=jnp.float32)
+    return (res[n:] + res[:n]).astype(jnp.bfloat16)
+
+
 def exchange_kernel(dims, xt_hbm, wi_ref, wo_ref, op_ref, yo_hbm, wt_hbm, gath, tt_ref,
                     xn, xb, xs, xl, ts, t2, sb1, sb2, rb, gsend, grecv, wi, wo, wf, wobs, obs_raw, obs_row, yp, cm, amat, cvec,
                     xsem, gssem, grsem, ssem, rsem, osem):
-    members, rows, columns, channels, patches, dev_rows, ens_size = dims
+    members, rows, columns, channels, patches, dev_rows, ens_size, done = dims
     units = patches * ens_size
     total_m = members * ens_size
     me = lax.axis_index("ens")
@@ -329,6 +342,15 @@
             trans = trans + (1.0 - jnp.sum(trans, axis=0, keepdims=True)) * (1.0 / total_m)
             tt_ref[patch + i] = trans[:, 0:total_m].T
 
+        @pl.when(patch < done)
+        def _():
+            def apply(i, carry):
+                lhs = stacked(tt_ref[patch + i // 4])
+                for c in range(columns):
+                    gath[patch + i // 4, i % 4, c] = transform(lhs, gath[patch + i // 4, i % 4, c])
+                return carry
+            lax.fori_loop(0, 8, apply, 0)
+
     def step(v, carry):
         @pl.when(v < units)
         def _():
@@ -364,22 +386,27 @@
     lax.fori_loop(0, patches, finish, 0)
 
 
-def update_kernel(tt_ref, g_ref, out_ref):
-    hi, mid, low = split3(tt_ref[pl.program_id(0)])
-    n = tt_ref.shape[1]
-    zero = jnp.zeros((n, n), jnp.float32)
-    lhs = jnp.concatenate([
-        jnp.concatenate([hi.astype(jnp.float32), mid.astype(jnp.float32)], axis=1),
-        jnp.concatenate([low.astype(jnp.float32), zero], axis=1)], axis=0).astype(jnp.bfloat16)
-
-    def row(r, carry):
-        for col in range(out_ref.shape[1]):
-            g = g_ref[pl.program_id(0), r, col]
-            res = jnp.dot(lhs, jnp.concatenate([g, g], axis=0), preferred_element_type=jnp.float32)
-            val = res[n:] + res[:n]
-            out_ref[r, col] = val[:, :out_ref.shape[3]].astype(jnp.bfloat16)
-        return carry
-    lax.fori_loop(0, out_ref.shape[0], row, 0)
+def update_kernel(done, tt_ref, g_ref, out_ref):
+    patch = pl.program_id(0)
+    channels = out_ref.shape[3]
+
+    @pl.when(patch < done)
+    def _():
+        def row(r, carry):
+            for col in range(out_ref.shape[1]):
+                out_ref[r, col] = g_ref[patch, r, col, :, 0:channels]
+            return carry
+        lax.fori_loop(0, out_ref.shape[0], row, 0)
+
+    @pl.when(patch >= done)
+    def _():
+        lhs = stacked(tt_ref[patch])
+
+        def row(r, carry):
+            for col in range(out_ref.shape[1]):
+                out_ref[r, col] = transform(lhs, g_ref[patch, r, col])[:, 0:channels]
+            return carry
+        lax.fori_loop(0, out_ref.shape[0], row, 0)
 
 
 def solution(mesh):
@@ -392,7 +419,8 @@
         dev_rows = rows // ens_size
         patches = dev_rows // 4
         units = patches * ens_size
-        dims = (members, rows, columns, channels, patches, dev_rows, ens_size)
+        done = patches - 2
+        dims = (members, rows, columns, channels, patches, dev_rows, ens_size, done)
         vmem = pl.BlockSpec(memory_space=pltpu.VMEM)
         anym = pl.BlockSpec(memory_space=pl.ANY)
         bf, f32 = jnp.bfloat16, jnp.float32
@@ -430,7 +458,7 @@
             compiler_params=pltpu.CompilerParams(collective_id=0, has_side_effects=True, vmem_limit_bytes=44 * 1024 * 1024),
         )(ens_state.transpose(0, 3, 2, 1), w_in, w_out.T, obs_op.T, obs_val, obs_wt)
         return pl.pallas_call(
-            update_kernel,
+            functools.partial(update_kernel, done),
             grid=(patches,),
             out_shape=jax.ShapeDtypeStruct((dev_rows, columns, total_m, channels), bf),
             in_specs=[vmem, vmem],

time: 218 us -> 211 us (0.968)
  Pallas kernels: 217 us -> 211 us
    pallas_call x1, Pallas kernels: 15.6 us -> 9.31 us  [local_step(): pl.pallas_call(functools.partial(update_kernel, done), grid=(patches,), o...]
where the time goes in v7:
time: 211 us
  Pallas kernels  211 us (100%)
    pallas_call x1, Pallas kernels, local_step(): pl.pallas_call(functools.partial(exchange_kernel, dims), out_shape=(pltpu...  202 us
    pallas_call x1, Pallas kernels, local_step(): pl.pallas_call(functools.partial(update_kernel, done), grid=(patches,), o...  9.31 us

profile of v7, /device:TPU:1, one launch (start us, length us, event | category | flops | bytes accessed | tf_op | source)
XLA Modules:
  0.0 210.9 jit_solution(14529761652125457196)
XLA Ops:
  0.0 201.6 %shard_map.64 = (bf16[8,4,16,64,256]{4,3,2,1,0:T(8,128)(2,1)S(1)}, f32[8,64,64]{2,1,0:T(8,128)S(1)}) custom-call(bf16[16,227,16,128]{3,2,1,0:T(8,128)(2,1)} %bitcast.3, bf16[454,512]{1,0:T(8,128)(2,1)} %wi_ref.1, bf16[227,512]{1,0:T(8,128)(2,1)} %bitcast.4, bf16[32,227]{1,0:T(8,128)(2,1)} %bitcast.5, f32[32,4,1,16,32]{4,3,2,1,0:T(8,128)} %yo_hbm.1, ...), custom_call_target="tpu_custom_call" | custom-call | tf_op jit(solution)/shard_map/pallas_call | solution.py:428
  201.6 9.3 %shard_map.65 = bf16[32,16,64,227]{3,2,1,0:T(8,128)(2,1)} custom-call(f32[8,64,64]{2,1,0:T(8,128)S(1)} %get-tuple-element.7.tt_ref, bf16[8,4,16,64,256]{4,3,2,1,0:T(8,128)(2,1)S(1)} %get-tuple-element.8.g_ref), custom_call_target="tpu_custom_call" | custom-call | tf_op jit(solution)/shard_map/pallas_call | solution.py:460

commit v8 on v7

--- a/solution.py
+++ b/solution.py
@@ -320,11 +320,11 @@
         amat[patch % 2, :, total_m:2 * total_m] = a_mat
         cvec[patch % 2] = jnp.broadcast_to(jnp.sum(csum, axis=1, keepdims=True), (total_m, 2 * total_m))
 
-    def solve(patch):
+    def solve(patch, slots):
         row = lax.broadcasted_iota(jnp.int32, (total_m, 2 * total_m), 0)
         col = lax.broadcasted_iota(jnp.int32, (total_m, 2 * total_m), 1)
         eye = ((row == col) | (row + total_m == col)).astype(jnp.float32)
-        mats = [amat[i] for i in range(2)]
+        mats = [amat[i] for i in slots]
         traces = [0.5 * jnp.sum(jnp.sum(a * eye, axis=0, keepdims=True), axis=1, keepdims=True) for a in mats]
 
         def newton(step, carry):
@@ -334,10 +334,10 @@
                 out.append((twin_dot(pair_lhs(y), pair_rhs(mix)), twin_dot(pair_lhs(mix), pair_rhs(z))))
             return tuple(out)
         pairs = lax.fori_loop(0, NS_STEPS, newton, tuple((a / t, eye) for a, t in zip(mats, traces)))
-        for i in range(2):
+        for i, slot in enumerate(slots):
             root = pairs[i][1] / jnp.sqrt(traces[i])
             left = pair_lhs(root)
-            wbar = twin_dot(left, pair_rhs(twin_dot(left, pair_rhs(cvec[i]))))
+            wbar = twin_dot(left, pair_rhs(twin_dot(left, pair_rhs(cvec[slot]))))
             trans = math.sqrt(total_m - 1.0) * root + wbar
             trans = trans + (1.0 - jnp.sum(trans, axis=0, keepdims=True)) * (1.0 / total_m)
             tt_ref[patch + i] = trans[:, 0:total_m].T
@@ -349,7 +349,7 @@
                 for c in range(columns):
                     gath[patch + i // 4, i % 4, c] = transform(lhs, gath[patch + i // 4, i % 4, c])
                 return carry
-            lax.fori_loop(0, 8, apply, 0)
+            lax.fori_loop(0, 4 * len(slots), apply, 0)
 
     def step(v, carry):
         @pl.when(v < units)
@@ -368,9 +368,13 @@
         def _():
             analysis(v // 4 - 3)
 
-        @pl.when((v >= 12) & (v % 8 == 0))
-        def _():
-            solve(v // 4 - 4)
+        @pl.when((v >= 12) & (v <= units) & (v % 8 == 0))
+        def _():
+            solve(v // 4 - 4, (0, 1))
+
+        @pl.when((v > units) & (v % 4 == 0))
+        def _():
+            solve(v // 4 - 3, ((v // 4 - 3) % 2,))
         return carry
     lax.fori_loop(0, units + 9, step, 0)
 
@@ -386,27 +390,31 @@
     lax.fori_loop(0, patches, finish, 0)
 
 
-def update_kernel(done, tt_ref, g_ref, out_ref):
-    patch = pl.program_id(0)
-    channels = out_ref.shape[3]
-
-    @pl.when(patch < done)
-    def _():
-        def row(r, carry):
-            for col in range(out_ref.shape[1]):
-                out_ref[r, col] = g_ref[patch, r, col, :, 0:channels]
-            return carry
-        lax.fori_loop(0, out_ref.shape[0], row, 0)
-
-    @pl.when(patch >= done)
-    def _():
-        lhs = stacked(tt_ref[patch])
-
-        def row(r, carry):
-            for col in range(out_ref.shape[1]):
-                out_ref[r, col] = transform(lhs, g_ref[patch, r, col])[:, 0:channels]
-            return carry
-        lax.fori_loop(0, out_ref.shape[0], row, 0)
+def update_kernel(done, tt_ref, g_ref, out_hbm, stage, sem):
+    channels = out_hbm.shape[3]
+
+    def copy(r):
+        return pltpu.make_async_copy(stage.at[r], out_hbm.at[r], sem.at[r])
+
+    def write(r, carry):
+        for col in range(stage.shape[1]):
+            stage[r, col] = g_ref[r // 4, r % 4, col, :, 0:channels]
+        copy(r).start()
+        return carry
+    lax.fori_loop(0, 4 * done, write, 0)
+
+    def last(r, carry):
+        lhs = stacked(tt_ref[r // 4])
+        for col in range(stage.shape[1]):
+            stage[r, col] = transform(lhs, g_ref[r // 4, r % 4, col])[:, 0:channels]
+        copy(r).start()
+        return carry
+    lax.fori_loop(4 * done, stage.shape[0], last, 0)
+
+    def drain(r, carry):
+        copy(r).wait()
+        return carry
+    lax.fori_loop(0, stage.shape[0], drain, 0)
 
 
 def solution(mesh):
@@ -419,7 +427,7 @@
         dev_rows = rows // ens_size
         patches = dev_rows // 4
         units = patches * ens_size
-        done = patches - 2
+        done = patches - 1
         dims = (members, rows, columns, channels, patches, dev_rows, ens_size, done)
         vmem = pl.BlockSpec(memory_space=pltpu.VMEM)
         anym = pl.BlockSpec(memory_space=pl.ANY)
@@ -459,11 +467,11 @@
         )(ens_state.transpose(0, 3, 2, 1), w_in, w_out.T, obs_op.T, obs_val, obs_wt)
         return pl.pallas_call(
             functools.partial(update_kernel, done),
-            grid=(patches,),
             out_shape=jax.ShapeDtypeStruct((dev_rows, columns, total_m, channels), bf),
             in_specs=[vmem, vmem],
-            out_specs=pl.BlockSpec((4, columns, total_m, channels), lambda p: (p, 0, 0, 0)),
-            compiler_params=pltpu.CompilerParams(dimension_semantics=("arbitrary",), vmem_limit_bytes=24 * 1024 * 1024),
+            out_specs=anym,
+            scratch_shapes=[pltpu.VMEM((dev_rows, columns, total_m, channels), bf), dma((dev_rows,))],
+            compiler_params=pltpu.CompilerParams(vmem_limit_bytes=24 * 1024 * 1024),
         )(pltpu.with_memory_space_constraint(trans, pltpu.VMEM), pltpu.with_memory_space_constraint(gathered, pltpu.VMEM))
 
     return jax.shard_map(local_step, mesh=mesh, in_specs=(P("ens", None, "dom", None), P(), P(), P(), obs_spec, obs_spec), out_specs=P("ens", "dom", None, None), check_vma=False)

time: 211 us -> 212 us (level)
  the two profiles are of different devices: /device:TPU:1 before, /device:TPU:0 now
where the time goes in v8:
time: 212 us; the launch traced here: 211 us
  Pallas kernels  211 us (100%)
    pallas_call x1, Pallas kernels, local_step(): pl.pallas_call(functools.partial(exchange_kernel, dims), out_shape=(pltpu...  205 us
    pallas_call x1, Pallas kernels, local_step(): pl.pallas_call(functools.partial(update_kernel, done), out_shape=jax.Shap...  6.12 us

profile of v8, /device:TPU:0, one launch (start us, length us, event | category | flops | bytes accessed | tf_op | source)
XLA Modules:
  0.0 211.2 jit_solution(5670951120299033629)
XLA Ops:
  0.0 205.0 %shard_map.64 = (bf16[8,4,16,64,256]{4,3,2,1,0:T(8,128)(2,1)S(1)}, f32[8,64,64]{2,1,0:T(8,128)S(1)}) custom-call(bf16[16,227,16,128]{3,2,1,0:T(8,128)(2,1)} %bitcast.3, bf16[454,512]{1,0:T(8,128)(2,1)} %wi_ref.1, bf16[227,512]{1,0:T(8,128)(2,1)} %bitcast.4, bf16[32,227]{1,0:T(8,128)(2,1)} %bitcast.5, f32[32,4,1,16,32]{4,3,2,1,0:T(8,128)} %yo_hbm.1, ...), custom_call_target="tpu_custom_call" | custom-call | tf_op jit(solution)/shard_map/pallas_call | solution.py:436
  205.0 6.1 %shard_map.65 = bf16[32,16,64,227]{3,2,1,0:T(8,128)(2,1)} custom-call(f32[8,64,64]{2,1,0:T(8,128)S(1)} %get-tuple-element.7.tt_ref, bf16[8,4,16,64,256]{4,3,2,1,0:T(8,128)(2,1)S(1)} %get-tuple-element.8.g_ref), custom_call_target="tpu_custom_call" | custom-call | tf_op jit(solution)/shard_map/pallas_call | solution.py:468

commit v9 on v8

--- a/solution.py
+++ b/solution.py
@@ -77,7 +77,7 @@
 
 
 def exchange_kernel(dims, xt_hbm, wi_ref, wo_ref, op_ref, yo_hbm, wt_hbm, gath, tt_ref,
-                    xn, xb, xs, xl, ts, t2, sb1, sb2, rb, gsend, grecv, wi, wo, wf, wobs, obs_raw, obs_row, yp, cm, amat, cvec,
+                    xn, xb, xs, xa, xl, ts, t2, sb1, sb2, rb, gsend, grecv, wi, wo, wf, wobs, obs_raw, obs_row, yp, cm, amat, cvec,
                     xsem, gssem, grsem, ssem, rsem, osem):
     members, rows, columns, channels, patches, dev_rows, ens_size, done = dims
     units = patches * ens_size
@@ -103,11 +103,11 @@
     def unit_copies(patch, dslot):
         dev = {"ens": dest_of(dslot)}
         first = pltpu.make_async_remote_copy(
-            src_ref=sb1.at[(patch % 3) * 3 + dslot], dst_ref=gath.at[patch, :, :, mine, pl.ds(0, 128)],
+            src_ref=sb1.at[(patch % 2) * 3 + dslot], dst_ref=gath.at[patch, :, :, mine, pl.ds(0, 128)],
             send_sem=ssem.at[patch, dslot, 0], recv_sem=rsem.at[patch, dslot, 0],
             device_id=dev, device_id_type=MESH)
         second = pltpu.make_async_remote_copy(
-            src_ref=sb2.at[(patch % 3) * 3 + dslot], dst_ref=rb.at[patch * 3 + dslot],
+            src_ref=sb2.at[(patch % 2) * 3 + dslot], dst_ref=rb.at[patch * 3 + dslot],
             send_sem=ssem.at[patch, dslot, 1], recv_sem=rsem.at[patch, dslot, 1],
             device_id=dev, device_id_type=MESH)
         return first, second
@@ -115,6 +115,7 @@
     obs_copies = [pltpu.make_async_copy(ref.at[pl.ds(me * patches, patches)], obs_raw.at[i], osem.at[i]) for i, ref in enumerate((yo_hbm, wt_hbm))]
 
     x_copy(0).start()
+    x_copy(1).start()
     for copy in obs_copies:
         copy.start()
     barrier = pltpu.get_barrier_semaphore()
@@ -122,7 +123,6 @@
         pl.semaphore_signal(barrier, inc=1, device_id={"ens": dest_of(dslot)}, device_id_type=MESH)
     pl.semaphore_signal(barrier, inc=1, device_id={"dom": 1 - mydom}, device_id_type=MESH)
 
-    xs[0, 1, 3, 17 * (channels % 32):544, :] = jnp.zeros((544 - 17 * (channels % 32), 128), jnp.float32)
     wf[...] = jnp.zeros_like(wf)
     wf[0:channels, :] = wo_ref[...].astype(jnp.float32)
     wo[...] = wf[0:CP, :].T.astype(jnp.bfloat16)
@@ -132,34 +132,52 @@
     wi[CP:2 * CP, :] = wf[channels:channels + CP, :].astype(jnp.bfloat16)
     turn = (lax.broadcasted_iota(jnp.int32, (128, 128), 0) == lax.broadcasted_iota(jnp.int32, (128, 128), 1)).astype(jnp.float32).astype(jnp.bfloat16)
 
-    def relayout(m, carry):
-        @pl.when(m + 1 < members)
-        def _():
-            x_copy(m + 1).start()
-        x_copy(m).wait()
-
-        def widen(b, c2):
-            for cc in range(32):
-                xs[0, b // 4, b % 4, 17 * cc:17 * cc + 16, :] = xn[m % 2, b * 32 + cc].astype(jnp.float32)
-            return c2
-        lax.fori_loop(0, channels // 32, widen, 0)
-        for cc in range(channels % 32):
-            xs[0, 1, 3, 17 * cc:17 * cc + 16, :] = xn[m % 2, channels - channels % 32 + cc].astype(jnp.float32)
-        for col in range(columns):
-            part = jnp.concatenate([xs[0, h, j, pl.ds(col, 32, stride=17), :] for h in range(2) for j in range(4)], axis=0)
-            out = lax.dot_general(turn, part.astype(jnp.bfloat16), NT, preferred_element_type=jnp.float32)
-            for h in range(2):
-                for j in range(4):
-                    xs[1, h, j, pl.ds(col, 32, stride=17), :] = out[32 * j:32 * j + 32, h * 128:h * 128 + 128]
-
-        def narrow(j, c2):
-            for rr in range(32):
-                for h in range(2):
-                    xb[m, 32 * j + rr, :, h * 128:h * 128 + 128] = xs[1, h, j, 17 * rr:17 * rr + 16, :].astype(jnp.bfloat16)
-            return c2
-        lax.fori_loop(0, 4, narrow, 0)
-        return carry
-    lax.fori_loop(0, members, relayout, 0)
+    wide = ([[xs.at[0, h, j] for j in range(4)] for h in range(2)],
+            [[xs.at[j // 2, h, 4 + j % 2] for j in range(4)] for h in range(2)])
+    turned = ([[xs.at[1, h, j] for j in range(4)] for h in range(2)],
+              [[xa.at[h, j] for j in range(4)] for h in range(2)])
+
+    def widen(odd, c):
+        wide[odd][c // 128][c // 32 % 4][17 * (c % 32):17 * (c % 32) + 16, :] = xn[odd, c].astype(jnp.float32)
+
+    def turn_column(odd, col):
+        part = jnp.concatenate([wide[odd][h][j][pl.ds(col, 32, stride=17), :] for h in range(2) for j in range(4)], axis=0)
+        out = lax.dot_general(turn, part.astype(jnp.bfloat16), NT, preferred_element_type=jnp.float32)
+        for h in range(2):
+            for j in range(4):
+                turned[odd][h][j][pl.ds(col, 32, stride=17), :] = out[32 * j:32 * j + 32, h * 128:h * 128 + 128]
+
+    def narrow(odd, m, row):
+        for h in range(2):
+            xb[m, row, :, h * 128:h * 128 + 128] = turned[odd][h][row // 32][17 * (row % 32):17 * (row % 32) + 16, :].astype(jnp.bfloat16)
+
+    def relayout(t, carry):
+        for odd in range(2):
+            m = 2 * t + odd
+
+            @pl.when(m + 2 < members)
+            def _():
+                x_copy(m + 2).start()
+
+            @pl.when(m + 1 < members)
+            def _():
+                x_copy(m + 1).wait()
+            for col in range(columns):
+                turn_column(odd, col)
+                for c in range(channels * col // columns, channels * (col + 1) // columns):
+                    widen(1 - odd, c)
+                for row in range(rows * col // columns, rows * (col + 1) // columns):
+                    narrow(1 - odd, jnp.maximum(m - 1, 0), row)
+        return carry
+    for ref in (wide[0][1][3], wide[1][1][3]):
+        ref[17 * (channels % 32):544, :] = jnp.zeros((544 - 17 * (channels % 32), 128), jnp.float32)
+    x_copy(0).wait()
+    for c in range(channels):
+        widen(0, c)
+    lax.fori_loop(0, members // 2, relayout, 0)
+
+    for row in range(rows):
+        narrow(1, members - 1, row)
     pl.semaphore_wait(barrier, 4)
 
     lane = lax.broadcasted_iota(jnp.int32, (members, 128), 1)
@@ -213,11 +231,11 @@
     def forecast(unit):
         patch, dslot = unit // ens_size, unit % ens_size
         slot = unit % 2
-        out_slot = jnp.where(dslot < 3, (patch % 3) * 3 + dslot, 9)
-
-        @pl.when((dslot < 3) & (patch >= 3))
-        def _():
-            for copy in unit_copies(patch - 3, dslot):
+        out_slot = jnp.where(dslot < 3, (patch % 2) * 3 + dslot, 6)
+
+        @pl.when((dslot < 3) & (patch >= 2))
+        def _():
+            for copy in unit_copies(patch - 2, dslot):
                 copy.wait_send()
         ghost_copy(unit).wait_recv()
 
@@ -269,7 +287,7 @@
         def _():
             def own(r, carry):
                 for col in range(columns):
-                    gath[patch, r, col, mine, 0:128] = sb1[9, r, col]
+                    gath[patch, r, col, mine, 0:128] = sb1[6, r, col]
                     gath[patch, r, col, mine, 128:256] = t2[r, col].astype(jnp.bfloat16)
                 return carry
             lax.fori_loop(0, 4, own, 0)
@@ -379,7 +397,7 @@
     lax.fori_loop(0, units + 9, step, 0)
 
     def finish(patch, carry):
-        @pl.when(patch >= patches - 3)
+        @pl.when(patch >= patches - 2)
         def _():
             for dslot in range(3):
                 for copy in unit_copies(patch, dslot):
@@ -443,11 +461,12 @@
                 pltpu.VMEM((2, channels, columns, rows), bf),
                 pltpu.VMEM((members, rows, columns, CP), bf),
                 pltpu.VMEM((2, 2, 6, 544, 128), f32),
+                pltpu.VMEM((2, 4, 544, 128), f32),
                 pltpu.VMEM((members * columns, 2 * CP), bf),
                 pltpu.VMEM((2, members * 17, 128), f32),
                 pltpu.VMEM((4, columns, members, 128), f32),
-                pltpu.VMEM((10, 4, columns, members, 128), bf),
-                pltpu.VMEM((9, 50, members, 128), bf),
+                pltpu.VMEM((7, 4, columns, members, 128), bf),
+                pltpu.VMEM((6, 50, members, 128), bf),
                 pltpu.VMEM((patches * 3, 50, members, 128), bf),
                 pltpu.VMEM((units, 2, 4, members, CP), bf),
                 pltpu.VMEM((units, 2, 4, members, CP), bf),
@@ -463,7 +482,7 @@
                 pltpu.VMEM((2, total_m, 2 * total_m), f32),
                 dma((2,)), dma((units,)), dma((units,)), dma((patches, 3, 2)), dma((patches, 3, 2)), dma((2,)),
             ],
-            compiler_params=pltpu.CompilerParams(collective_id=0, has_side_effects=True, vmem_limit_bytes=44 * 1024 * 1024),
+            compiler_params=pltpu.CompilerParams(collective_id=0, has_side_effects=True, vmem_limit_bytes=46 * 1024 * 1024),
         )(ens_state.transpose(0, 3, 2, 1), w_in, w_out.T, obs_op.T, obs_val, obs_wt)
         return pl.pallas_call(
             functools.partial(update_kernel, done),

time: 212 us -> 210 us (level)
  no operation moved by 1% of the time
where the time goes in v9:
time: 210 us
  Pallas kernels  210 us (100%)
    pallas_call x1, Pallas kernels, local_step(): pl.pallas_call(functools.partial(exchange_kernel, dims), out_shape=(pltpu...  204 us
    pallas_call x1, Pallas kernels, local_step(): pl.pallas_call(functools.partial(update_kernel, done), out_shape=jax.Shap...  6.12 us

profile of v9, /device:TPU:0, one launch (start us, length us, event | category | flops | bytes accessed | tf_op | source)
XLA Modules:
  0.0 209.9 jit_solution(10010162494109878368)
XLA Ops:
  0.0 203.8 %shard_map.64 = (bf16[8,4,16,64,256]{4,3,2,1,0:T(8,128)(2,1)S(1)}, f32[8,64,64]{2,1,0:T(8,128)S(1)}) custom-call(bf16[16,227,16,128]{3,2,1,0:T(8,128)(2,1)} %bitcast.3, bf16[454,512]{1,0:T(8,128)(2,1)} %wi_ref.1, bf16[227,512]{1,0:T(8,128)(2,1)} %bitcast.4, bf16[32,227]{1,0:T(8,128)(2,1)} %bitcast.5, f32[32,4,1,16,32]{4,3,2,1,0:T(8,128)} %yo_hbm.1, ...), custom_call_target="tpu_custom_call" | custom-call | tf_op jit(solution)/shard_map/pallas_call | solution.py:454
  203.8 6.1 %shard_map.65 = bf16[32,16,64,227]{3,2,1,0:T(8,128)(2,1)} custom-call(f32[8,64,64]{2,1,0:T(8,128)S(1)} %get-tuple-element.7.tt_ref, bf16[8,4,16,64,256]{4,3,2,1,0:T(8,128)(2,1)S(1)} %get-tuple-element.8.g_ref), custom_call_target="tpu_custom_call" | custom-call | tf_op jit(solution)/shard_map/pallas_call | solution.py:487

commit v10 on v9

--- a/solution.py
+++ b/solution.py
@@ -386,13 +386,9 @@
         def _():
             analysis(v // 4 - 3)
 
-        @pl.when((v >= 12) & (v <= units) & (v % 8 == 0))
+        @pl.when((v >= 12) & (v % 8 == 0))
         def _():
             solve(v // 4 - 4, (0, 1))
-
-        @pl.when((v > units) & (v % 4 == 0))
-        def _():
-            solve(v // 4 - 3, ((v // 4 - 3) % 2,))
         return carry
     lax.fori_loop(0, units + 9, step, 0)
 
@@ -445,7 +441,7 @@
         dev_rows = rows // ens_size
         patches = dev_rows // 4
         units = patches * ens_size
-        done = patches - 1
+        done = patches - 2
         dims = (members, rows, columns, channels, patches, dev_rows, ens_size, done)
         vmem = pl.BlockSpec(memory_space=pltpu.VMEM)
         anym = pl.BlockSpec(memory_space=pl.ANY)

time: 210 us -> 207 us (0.986)
  the two profiles are of different devices: /device:TPU:0 before, /device:TPU:1 now
where the time goes in v10:
time: 207 us
  Pallas kernels  207 us (100%)
    pallas_call x1, Pallas kernels, local_step(): pl.pallas_call(functools.partial(exchange_kernel, dims), out_shape=(pltpu...  201 us
    pallas_call x1, Pallas kernels, local_step(): pl.pallas_call(functools.partial(update_kernel, done), out_shape=jax.Shap...  6.12 us

profile of v10, /device:TPU:1, one launch (start us, length us, event | category | flops | bytes accessed | tf_op | source)
XLA Modules:
  0.0 206.7 jit_solution(16589517916312578159)
XLA Ops:
  0.0 200.6 %shard_map.64 = (bf16[8,4,16,64,256]{4,3,2,1,0:T(8,128)(2,1)S(1)}, f32[8,64,64]{2,1,0:T(8,128)S(1)}) custom-call(bf16[16,227,16,128]{3,2,1,0:T(8,128)(2,1)} %bitcast.3, bf16[454,512]{1,0:T(8,128)(2,1)} %wi_ref.1, bf16[227,512]{1,0:T(8,128)(2,1)} %bitcast.4, bf16[32,227]{1,0:T(8,128)(2,1)} %bitcast.5, f32[32,4,1,16,32]{4,3,2,1,0:T(8,128)} %yo_hbm.1, ...), custom_call_target="tpu_custom_call" | custom-call | tf_op jit(solution)/shard_map/pallas_call | solution.py:450
  200.6 6.1 %shard_map.65 = bf16[32,16,64,227]{3,2,1,0:T(8,128)(2,1)} custom-call(f32[8,64,64]{2,1,0:T(8,128)S(1)} %get-tuple-element.7.tt_ref, bf16[8,4,16,64,256]{4,3,2,1,0:T(8,128)(2,1)S(1)} %get-tuple-element.8.g_ref), custom_call_target="tpu_custom_call" | custom-call | tf_op jit(solution)/shard_map/pallas_call | solution.py:483

commit v11 on v10

--- a/solution.py
+++ b/solution.py
@@ -43,24 +43,19 @@
     return (small + (by_mid[:n] + by_hi[n:2 * n])) + by_hi[:n]
 
 
-def pair_lhs(a):
-    hi, mid, low = split3(a)
-    first = lax.broadcasted_iota(jnp.int32, a.shape, 1) < a.shape[1] // 2
-    hi, mid, low = (v.astype(jnp.float32) for v in (hi, mid, low))
-    lead = jnp.where(first, hi, mid).astype(jnp.bfloat16)
-    return jnp.concatenate([lead, lead, jnp.where(first, hi, low).astype(jnp.bfloat16)], axis=1)
-
-
-def pair_rhs(b):
-    hi, mid, low = split3(b)
-    return jnp.concatenate([hi, hi, mid, mid, low, hi], axis=0)
-
-
-def twin_dot(lhs, rhs):
-    k = rhs.shape[1]
-    acc = jnp.dot(lhs[:, 2*k:], rhs[2*k:], preferred_element_type=jnp.float32)
-    acc = acc + jnp.dot(lhs[:, k:2*k], rhs[k:2*k], preferred_element_type=jnp.float32)
-    return acc + jnp.dot(lhs[:, :k], rhs[:k], preferred_element_type=jnp.float32)
+def packed_dot(a, b, left, right):
+    ah, am, al = split3(a)
+    bh, bm, bl = split3(b)
+    n = a.shape[0]
+
+    def dot(u, v):
+        blocks = jnp.concatenate([v * left, v * right], axis=0)
+        return jnp.dot(u, blocks, preferred_element_type=jnp.float32)
+    by_hi = dot(jnp.concatenate([ah, am, al], axis=0), bh)
+    by_mid = dot(jnp.concatenate([ah, am], axis=0), bm)
+    by_low = dot(ah, bl)
+    small = (by_low + by_hi[2 * n:]) + by_mid[n:]
+    return (small + (by_mid[:n] + by_hi[n:2 * n])) + by_hi[:n]
 
 
 def stacked(t):
@@ -338,27 +333,30 @@
         amat[patch % 2, :, total_m:2 * total_m] = a_mat
         cvec[patch % 2] = jnp.broadcast_to(jnp.sum(csum, axis=1, keepdims=True), (total_m, 2 * total_m))
 
-    def solve(patch, slots):
+    def solve(patch):
         row = lax.broadcasted_iota(jnp.int32, (total_m, 2 * total_m), 0)
         col = lax.broadcasted_iota(jnp.int32, (total_m, 2 * total_m), 1)
         eye = ((row == col) | (row + total_m == col)).astype(jnp.float32)
-        mats = [amat[i] for i in slots]
-        traces = [0.5 * jnp.sum(jnp.sum(a * eye, axis=0, keepdims=True), axis=1, keepdims=True) for a in mats]
+        first = col < total_m
+        left = first.astype(jnp.float32).astype(jnp.bfloat16)
+        right = (col >= total_m).astype(jnp.float32).astype(jnp.bfloat16)
+        mats = jnp.where(first, amat[0], amat[1])
+        diag = jnp.sum(mats * eye, axis=0, keepdims=True)
+        trace = jnp.where(first[0:1], jnp.sum(jnp.where(first[0:1], diag, 0.0), axis=1, keepdims=True),
+                          jnp.sum(jnp.where(first[0:1], 0.0, diag), axis=1, keepdims=True))
 
         def newton(step, carry):
-            out = []
-            for y, z in carry:
-                mix = 1.5 * eye - 0.5 * twin_dot(pair_lhs(z), pair_rhs(y))
-                out.append((twin_dot(pair_lhs(y), pair_rhs(mix)), twin_dot(pair_lhs(mix), pair_rhs(z))))
-            return tuple(out)
-        pairs = lax.fori_loop(0, NS_STEPS, newton, tuple((a / t, eye) for a, t in zip(mats, traces)))
-        for i, slot in enumerate(slots):
-            root = pairs[i][1] / jnp.sqrt(traces[i])
-            left = pair_lhs(root)
-            wbar = twin_dot(left, pair_rhs(twin_dot(left, pair_rhs(cvec[slot]))))
-            trans = math.sqrt(total_m - 1.0) * root + wbar
-            trans = trans + (1.0 - jnp.sum(trans, axis=0, keepdims=True)) * (1.0 / total_m)
-            tt_ref[patch + i] = trans[:, 0:total_m].T
+            y, z = carry
+            mix = 1.5 * eye - 0.5 * packed_dot(z, y, left, right)
+            return packed_dot(y, mix, left, right), packed_dot(mix, z, left, right)
+        _, inv = lax.fori_loop(0, NS_STEPS, newton, (mats / trace, eye))
+        root = inv / jnp.sqrt(trace)
+        wbar = packed_dot(root, packed_dot(root, jnp.where(first, cvec[0], cvec[1]), left, right), left, right)
+        trans = math.sqrt(total_m - 1.0) * root + wbar
+        trans = trans + (1.0 - jnp.sum(trans, axis=0, keepdims=True)) * (1.0 / total_m)
+        both = trans.T
+        tt_ref[patch] = both[0:total_m]
+        tt_ref[patch + 1] = both[total_m:2 * total_m]
 
         @pl.when(patch < done)
         def _():
@@ -367,7 +365,7 @@
                 for c in range(columns):
                     gath[patch + i // 4, i % 4, c] = transform(lhs, gath[patch + i // 4, i % 4, c])
                 return carry
-            lax.fori_loop(0, 4 * len(slots), apply, 0)
+            lax.fori_loop(0, 8, apply, 0)
 
     def step(v, carry):
         @pl.when(v < units)
@@ -388,7 +386,7 @@
 
         @pl.when((v >= 12) & (v % 8 == 0))
         def _():
-            solve(v // 4 - 4, (0, 1))
+            solve(v // 4 - 4)
         return carry
     lax.fori_loop(0, units + 9, step, 0)
 

time: 207 us -> 203 us (0.981)
  Pallas kernels: 207 us -> 203 us
    pallas_call x1, Pallas kernels: 201 us -> 197 us  [local_step(): pl.pallas_call(functools.partial(exchange_kernel, dims), out_shape=(pltpu...]
where the time goes in v11:
time: 203 us
  Pallas kernels  203 us (100%)
    pallas_call x1, Pallas kernels, local_step(): pl.pallas_call(functools.partial(exchange_kernel, dims), out_shape=(pltpu...  197 us
    pallas_call x1, Pallas kernels, local_step(): pl.pallas_call(functools.partial(update_kernel, done), out_shape=jax.Shap...  6.12 us

profile of v11, /device:TPU:1, one launch (start us, length us, event | category | flops | bytes accessed | tf_op | source)
XLA Modules:
  0.0 202.9 jit_solution(10765592533483643055)
XLA Ops:
  0.0 196.8 %shard_map.64 = (bf16[8,4,16,64,256]{4,3,2,1,0:T(8,128)(2,1)S(1)}, f32[8,64,64]{2,1,0:T(8,128)S(1)}) custom-call(bf16[16,227,16,128]{3,2,1,0:T(8,128)(2,1)} %bitcast.3, bf16[454,512]{1,0:T(8,128)(2,1)} %wi_ref.1, bf16[227,512]{1,0:T(8,128)(2,1)} %bitcast.4, bf16[32,227]{1,0:T(8,128)(2,1)} %bitcast.5, f32[32,4,1,16,32]{4,3,2,1,0:T(8,128)} %yo_hbm.1, ...), custom_call_target="tpu_custom_call" | custom-call | tf_op jit(solution)/shard_map/pallas_call | solution.py:448
  196.8 6.1 %shard_map.65 = bf16[32,16,64,227]{3,2,1,0:T(8,128)(2,1)} custom-call(f32[8,64,64]{2,1,0:T(8,128)S(1)} %get-tuple-element.7.tt_ref, bf16[8,4,16,64,256]{4,3,2,1,0:T(8,128)(2,1)S(1)} %get-tuple-element.8.g_ref), custom_call_target="tpu_custom_call" | custom-call | tf_op jit(solution)/shard_map/pallas_call | solution.py:481

commit v12 on v11

--- a/solution.py
+++ b/solution.py
@@ -95,17 +95,24 @@
             src_ref=gsend.at[unit], dst_ref=grecv.at[unit], send_sem=gssem.at[unit], recv_sem=grsem.at[unit],
             device_id={"dom": 1 - mydom}, device_id_type=MESH)
 
-    def unit_copies(patch, dslot):
+    def pair_copies(patch, dslot, pair):
         dev = {"ens": dest_of(dslot)}
+        slot, box = (patch % 2) * 3 + dslot, patch * 3 + dslot
+        two, tiles = pl.ds(pair * 2, 2), pl.ds(pair * 25, 25)
         first = pltpu.make_async_remote_copy(
-            src_ref=sb1.at[(patch % 2) * 3 + dslot], dst_ref=gath.at[patch, :, :, mine, pl.ds(0, 128)],
-            send_sem=ssem.at[patch, dslot, 0], recv_sem=rsem.at[patch, dslot, 0],
+            src_ref=sb1.at[slot, two], dst_ref=gath.at[patch, two, :, mine, pl.ds(0, 128)],
+            send_sem=ssem.at[patch, dslot, pair * 2], recv_sem=rsem.at[patch, dslot, pair * 2],
             device_id=dev, device_id_type=MESH)
         second = pltpu.make_async_remote_copy(
-            src_ref=sb2.at[(patch % 2) * 3 + dslot], dst_ref=rb.at[patch * 3 + dslot],
-            send_sem=ssem.at[patch, dslot, 1], recv_sem=rsem.at[patch, dslot, 1],
+            src_ref=sb2.at[slot, tiles], dst_ref=rb.at[box, tiles],
+            send_sem=ssem.at[patch, dslot, pair * 2 + 1], recv_sem=rsem.at[patch, dslot, pair * 2 + 1],
             device_id=dev, device_id_type=MESH)
         return first, second
+
+    def wait_sent(patch, dslot):
+        for pair in range(2):
+            for copy in pair_copies(patch, dslot, pair):
+                copy.wait_send()
 
     obs_copies = [pltpu.make_async_copy(ref.at[pl.ds(me * patches, patches)], obs_raw.at[i], osem.at[i]) for i, ref in enumerate((yo_hbm, wt_hbm))]
 
@@ -230,8 +237,7 @@
 
         @pl.when((dslot < 3) & (patch >= 2))
         def _():
-            for copy in unit_copies(patch - 2, dslot):
-                copy.wait_send()
+            wait_sent(patch - 2, dslot)
         ghost_copy(unit).wait_recv()
 
         def block(r, carry):
@@ -259,39 +265,45 @@
                 sb1[out_slot, r, col] = ts[0, pl.ds(col, members, stride=17), :].astype(jnp.bfloat16)
                 t2[r, col] = ts[1, pl.ds(col, members, stride=17), :]
             return carry
-        lax.fori_loop(0, 4, block, 0)
-
-        @pl.when(dslot < 3)
-        def _():
-            def pack(pair, carry):
-                left = jnp.zeros((members, 128), jnp.float32)
-                for k in range(8):
-                    r, c0 = pair * 2 + k // 4, (k % 4) * 4
-                    v = [t2[r, c0 + i] for i in range(4)]
-                    for i in range(3):
-                        sb2[out_slot, pair * 25 + k * 3 + i] = jnp.where(lane < 96, v[i], pltpu.roll(v[3], 96 - 32 * i, 1)).astype(jnp.bfloat16)
-                    for i in range(4):
-                        left = left + pltpu.roll(jnp.where(lane >= 96, v[i], 0.0), (32 + 3 * (4 * k + i)) % 128, 1)
-                sb2[out_slot, pair * 25 + 24] = left.astype(jnp.bfloat16)
-                return carry
-            lax.fori_loop(0, 2, pack, 0)
-            for copy in unit_copies(patch, dslot):
-                copy.start()
-
-        @pl.when(dslot == 3)
-        def _():
-            def own(r, carry):
-                for col in range(columns):
-                    gath[patch, r, col, mine, 0:128] = sb1[6, r, col]
-                    gath[patch, r, col, mine, 128:256] = t2[r, col].astype(jnp.bfloat16)
-                return carry
-            lax.fori_loop(0, 4, own, 0)
+
+        def pack(pair):
+            left = jnp.zeros((members, 128), jnp.float32)
+            for k in range(8):
+                r, c0 = pair * 2 + k // 4, (k % 4) * 4
+                v = [t2[r, c0 + i] for i in range(4)]
+                for i in range(3):
+                    sb2[out_slot, pair * 25 + k * 3 + i] = jnp.where(lane < 96, v[i], pltpu.roll(v[3], 96 - 32 * i, 1)).astype(jnp.bfloat16)
+                for i in range(4):
+                    left = left + pltpu.roll(jnp.where(lane >= 96, v[i], 0.0), (32 + 3 * (4 * k + i)) % 128, 1)
+            sb2[out_slot, pair * 25 + 24] = left.astype(jnp.bfloat16)
+
+        def half_unit(pair, carry):
+            lax.fori_loop(pair * 2, pair * 2 + 2, block, 0)
+
+            @pl.when(dslot < 3)
+            def _():
+                pack(pair)
+                for copy in pair_copies(patch, dslot, pair):
+                    copy.start()
+
+            @pl.when(dslot == 3)
+            def _():
+                def own(r, c2):
+                    for col in range(columns):
+                        gath[patch, r, col, mine, 0:128] = sb1[6, r, col]
+                        gath[patch, r, col, mine, 128:256] = t2[r, col].astype(jnp.bfloat16)
+                    return c2
+                lax.fori_loop(pair * 2, pair * 2 + 2, own, 0)
+            return carry
+        lax.fori_loop(0, 2, half_unit, 0)
 
     def unpack(patch, dslot):
         src = pl.ds(pl.multiple_of(dest_of(dslot) * members, members), members)
         box = patch * 3 + dslot
 
         def half(pair, carry):
+            for copy in pair_copies(patch, dslot, pair):
+                copy.wait_recv()
             left = rb[box, pair * 25 + 24].astype(jnp.float32)
             for k in range(8):
                 r, c0 = pair * 2 + k // 4, (k % 4) * 4
@@ -307,8 +319,6 @@
 
     def analysis(patch):
         def arrive(dslot, carry):
-            for copy in unit_copies(patch, dslot):
-                copy.wait_recv()
             unpack(patch, dslot)
             return carry
         lax.fori_loop(0, 3, lambda i, c: arrive(2 - i, c), 0)
@@ -345,11 +355,17 @@
         trace = jnp.where(first[0:1], jnp.sum(jnp.where(first[0:1], diag, 0.0), axis=1, keepdims=True),
                           jnp.sum(jnp.where(first[0:1], 0.0, diag), axis=1, keepdims=True))
 
+        def mixer(z, y):
+            return 1.5 * eye - 0.5 * packed_dot(z, y, left, right)
+
         def newton(step, carry):
             y, z = carry
-            mix = 1.5 * eye - 0.5 * packed_dot(z, y, left, right)
+            mix = mixer(z, y)
             return packed_dot(y, mix, left, right), packed_dot(mix, z, left, right)
-        _, inv = lax.fori_loop(0, NS_STEPS, newton, (mats / trace, eye))
+        scaled = mats / trace
+        mix = 1.5 * eye - 0.5 * scaled
+        y, z = lax.fori_loop(1, NS_STEPS - 1, newton, (packed_dot(scaled, mix, left, right), mix))
+        inv = packed_dot(mixer(z, y), z, left, right)
         root = inv / jnp.sqrt(trace)
         wbar = packed_dot(root, packed_dot(root, jnp.where(first, cvec[0], cvec[1]), left, right), left, right)
         trans = math.sqrt(total_m - 1.0) * root + wbar
@@ -376,7 +392,7 @@
         def _():
             forecast(v - 1)
 
-        @pl.when(v == 3)
+        @pl.when(v == 0)
         def _():
             setup()
 
@@ -394,8 +410,7 @@
         @pl.when(patch >= patches - 2)
         def _():
             for dslot in range(3):
-                for copy in unit_copies(patch, dslot):
-                    copy.wait_send()
+                wait_sent(patch, dslot)
         for dslot in range(4):
             ghost_copy(patch * 4 + dslot).wait_send()
         return carry
@@ -474,7 +489,7 @@
                 pltpu.VMEM((8, total_m, CP), f32),
                 pltpu.VMEM((2, total_m, 2 * total_m), f32),
                 pltpu.VMEM((2, total_m, 2 * total_m), f32),
-                dma((2,)), dma((units,)), dma((units,)), dma((patches, 3, 2)), dma((patches, 3, 2)), dma((2,)),
+                dma((2,)), dma((units,)), dma((units,)), dma((patches, 3, 4)), dma((patches, 3, 4)), dma((2,)),
             ],
             compiler_params=pltpu.CompilerParams(collective_id=0, has_side_effects=True, vmem_limit_bytes=46 * 1024 * 1024),
         )(ens_state.transpose(0, 3, 2, 1), w_in, w_out.T, obs_op.T, obs_val, obs_wt)

time: 203 us -> 203 us (level)
  no operation moved by 1% of the time
where the time goes in v12:
time: 203 us; the launch traced here: 202 us
  Pallas kernels  202 us (100%)
    pallas_call x1, Pallas kernels, local_step(): pl.pallas_call(functools.partial(exchange_kernel, dims), out_shape=(pltpu...  196 us
    pallas_call x1, Pallas kernels, local_step(): pl.pallas_call(functools.partial(update_kernel, done), out_shape=jax.Shap...  6.12 us

profile of v12, /device:TPU:1, one launch (start us, length us, event | category | flops | bytes accessed | tf_op | source)
XLA Modules:
  0.0 202.2 jit_solution(12155920488891589339)
XLA Ops:
  0.0 196.1 %shard_map.64 = (bf16[8,4,16,64,256]{4,3,2,1,0:T(8,128)(2,1)S(1)}, f32[8,64,64]{2,1,0:T(8,128)S(1)}) custom-call(bf16[16,227,16,128]{3,2,1,0:T(8,128)(2,1)} %bitcast.3, bf16[454,512]{1,0:T(8,128)(2,1)} %wi_ref.1, bf16[227,512]{1,0:T(8,128)(2,1)} %bitcast.4, bf16[32,227]{1,0:T(8,128)(2,1)} %bitcast.5, f32[32,4,1,16,32]{4,3,2,1,0:T(8,128)} %yo_hbm.1, ...), custom_call_target="tpu_custom_call" | custom-call | tf_op jit(solution)/shard_map/pallas_call | solution.py:463
  196.1 6.1 %shard_map.65 = bf16[32,16,64,227]{3,2,1,0:T(8,128)(2,1)} custom-call(f32[8,64,64]{2,1,0:T(8,128)S(1)} %get-tuple-element.7.tt_ref, bf16[8,4,16,64,256]{4,3,2,1,0:T(8,128)(2,1)S(1)} %get-tuple-element.8.g_ref), custom_call_target="tpu_custom_call" | custom-call | tf_op jit(solution)/shard_map/pallas_call | solution.py:496

commit v13 on v12

--- a/solution.py
+++ b/solution.py
@@ -92,12 +92,12 @@
 
     def ghost_copy(unit):
         return pltpu.make_async_remote_copy(
-            src_ref=gsend.at[unit], dst_ref=grecv.at[unit], send_sem=gssem.at[unit], recv_sem=grsem.at[unit],
+            src_ref=gsend.at[unit % 8], dst_ref=grecv.at[unit], send_sem=gssem.at[unit], recv_sem=grsem.at[unit],
             device_id={"dom": 1 - mydom}, device_id_type=MESH)
 
     def pair_copies(patch, dslot, pair):
         dev = {"ens": dest_of(dslot)}
-        slot, box = (patch % 2) * 3 + dslot, patch * 3 + dslot
+        slot, box = (patch % 4) * 3 + dslot, patch * 3 + dslot
         two, tiles = pl.ds(pair * 2, 2), pl.ds(pair * 25, 25)
         first = pltpu.make_async_remote_copy(
             src_ref=sb1.at[slot, two], dst_ref=gath.at[patch, two, :, mine, pl.ds(0, 128)],
@@ -222,10 +222,14 @@
             return carry
         lax.fori_loop(0, 6, convert, 0)
 
+        @pl.when(unit >= 8)
+        def _():
+            ghost_copy(unit - 8).wait_send()
+
         def edges(r, carry):
             for h in range(2):
-                gsend[unit, 0, r, :, h * 128:h * 128 + 128] = xs[slot, h, r + 1, pl.ds(23, members, stride=33), :].astype(jnp.bfloat16)
-                gsend[unit, 1, r, :, h * 128:h * 128 + 128] = xs[slot, h, r + 1, pl.ds(8, members, stride=33), :].astype(jnp.bfloat16)
+                gsend[unit % 8, 0, r, :, h * 128:h * 128 + 128] = xs[slot, h, r + 1, pl.ds(23, members, stride=33), :].astype(jnp.bfloat16)
+                gsend[unit % 8, 1, r, :, h * 128:h * 128 + 128] = xs[slot, h, r + 1, pl.ds(8, members, stride=33), :].astype(jnp.bfloat16)
             return carry
         lax.fori_loop(0, 4, edges, 0)
         ghost_copy(unit).start()
@@ -233,11 +237,11 @@
     def forecast(unit):
         patch, dslot = unit // ens_size, unit % ens_size
         slot = unit % 2
-        out_slot = jnp.where(dslot < 3, (patch % 2) * 3 + dslot, 6)
-
-        @pl.when((dslot < 3) & (patch >= 2))
-        def _():
-            wait_sent(patch - 2, dslot)
+        out_slot = jnp.where(dslot < 3, (patch % 4) * 3 + dslot, 12)
+
+        @pl.when((dslot < 3) & (patch >= 4))
+        def _():
+            wait_sent(patch - 4, dslot)
         ghost_copy(unit).wait_recv()
 
         def block(r, carry):
@@ -290,7 +294,7 @@
             def _():
                 def own(r, c2):
                     for col in range(columns):
-                        gath[patch, r, col, mine, 0:128] = sb1[6, r, col]
+                        gath[patch, r, col, mine, 0:128] = sb1[12, r, col]
                         gath[patch, r, col, mine, 128:256] = t2[r, col].astype(jnp.bfloat16)
                     return c2
                 lax.fori_loop(pair * 2, pair * 2 + 2, own, 0)
@@ -396,23 +400,25 @@
         def _():
             setup()
 
-        @pl.when((v >= 12) & (v % 4 == 0))
-        def _():
-            analysis(v // 4 - 3)
-
-        @pl.when((v >= 12) & (v % 8 == 0))
-        def _():
-            solve(v // 4 - 4)
+        @pl.when((v >= 16) & (v % 4 == 0))
+        def _():
+            analysis(v // 4 - 4)
+
+        @pl.when((v >= 16) & (v % 8 == 4))
+        def _():
+            solve(v // 4 - 5)
         return carry
-    lax.fori_loop(0, units + 9, step, 0)
+    lax.fori_loop(0, units + 13, step, 0)
 
     def finish(patch, carry):
-        @pl.when(patch >= patches - 2)
+        @pl.when(patch >= patches - 4)
         def _():
             for dslot in range(3):
                 wait_sent(patch, dslot)
-        for dslot in range(4):
-            ghost_copy(patch * 4 + dslot).wait_send()
+        @pl.when(patch >= patches - 2)
+        def _():
+            for dslot in range(4):
+                ghost_copy(patch * 4 + dslot).wait_send()
         return carry
     lax.fori_loop(0, patches, finish, 0)
 
@@ -474,10 +480,10 @@
                 pltpu.VMEM((members * columns, 2 * CP), bf),
                 pltpu.VMEM((2, members * 17, 128), f32),
                 pltpu.VMEM((4, columns, members, 128), f32),
-                pltpu.VMEM((7, 4, columns, members, 128), bf),
-                pltpu.VMEM((6, 50, members, 128), bf),
+                pltpu.VMEM((13, 4, columns, members, 128), bf),
+                pltpu.VMEM((12, 50, members, 128), bf),
                 pltpu.VMEM((patches * 3, 50, members, 128), bf),
-                pltpu.VMEM((units, 2, 4, members, CP), bf),
+                pltpu.VMEM((8, 2, 4, members, CP), bf),
                 pltpu.VMEM((units, 2, 4, members, CP), bf),
                 pltpu.VMEM((2 * CP, 512), bf),
                 pltpu.VMEM((512, CP), bf),

time: 203 us -> 203 us (level)
  no operation moved by 1% of the time
where the time goes in v13:
time: 203 us; the launch traced here: 202 us
  Pallas kernels  202 us (100%)
    pallas_call x1, Pallas kernels, local_step(): pl.pallas_call(functools.partial(exchange_kernel, dims), out_shape=(pltpu...  196 us
    pallas_call x1, Pallas kernels, local_step(): pl.pallas_call(functools.partial(update_kernel, done), out_shape=jax.Shap...  6.12 us

profile of v13, /device:TPU:1, one launch (start us, length us, event | category | flops | bytes accessed | tf_op | source)
XLA Modules:
  0.0 202.2 jit_solution(1875606611156213424)
XLA Ops:
  0.0 196.1 %shard_map.64 = (bf16[8,4,16,64,256]{4,3,2,1,0:T(8,128)(2,1)S(1)}, f32[8,64,64]{2,1,0:T(8,128)S(1)}) custom-call(bf16[16,227,16,128]{3,2,1,0:T(8,128)(2,1)} %bitcast.3, bf16[454,512]{1,0:T(8,128)(2,1)} %wi_ref.1, bf16[227,512]{1,0:T(8,128)(2,1)} %bitcast.4, bf16[32,227]{1,0:T(8,128)(2,1)} %bitcast.5, f32[32,4,1,16,32]{4,3,2,1,0:T(8,128)} %yo_hbm.1, ...), custom_call_target="tpu_custom_call" | custom-call | tf_op jit(solution)/shard_map/pallas_call | solution.py:469
  196.1 6.1 %shard_map.65 = bf16[32,16,64,227]{3,2,1,0:T(8,128)(2,1)} custom-call(f32[8,64,64]{2,1,0:T(8,128)S(1)} %get-tuple-element.7.tt_ref, bf16[8,4,16,64,256]{4,3,2,1,0:T(8,128)(2,1)S(1)} %get-tuple-element.8.g_ref), custom_call_target="tpu_custom_call" | custom-call | tf_op jit(solution)/shard_map/pallas_call | solution.py:502

commit v14 on v12

--- a/solution.py
+++ b/solution.py
@@ -92,7 +92,7 @@
 
     def ghost_copy(unit):
         return pltpu.make_async_remote_copy(
-            src_ref=gsend.at[unit], dst_ref=grecv.at[unit], send_sem=gssem.at[unit], recv_sem=grsem.at[unit],
+            src_ref=gsend.at[unit % 8], dst_ref=grecv.at[unit], send_sem=gssem.at[unit], recv_sem=grsem.at[unit],
             device_id={"dom": 1 - mydom}, device_id_type=MESH)
 
     def pair_copies(patch, dslot, pair):
@@ -222,10 +222,14 @@
             return carry
         lax.fori_loop(0, 6, convert, 0)
 
+        @pl.when(unit >= 8)
+        def _():
+            ghost_copy(unit - 8).wait_send()
+
         def edges(r, carry):
             for h in range(2):
-                gsend[unit, 0, r, :, h * 128:h * 128 + 128] = xs[slot, h, r + 1, pl.ds(23, members, stride=33), :].astype(jnp.bfloat16)
-                gsend[unit, 1, r, :, h * 128:h * 128 + 128] = xs[slot, h, r + 1, pl.ds(8, members, stride=33), :].astype(jnp.bfloat16)
+                gsend[unit % 8, 0, r, :, h * 128:h * 128 + 128] = xs[slot, h, r + 1, pl.ds(23, members, stride=33), :].astype(jnp.bfloat16)
+                gsend[unit % 8, 1, r, :, h * 128:h * 128 + 128] = xs[slot, h, r + 1, pl.ds(8, members, stride=33), :].astype(jnp.bfloat16)
             return carry
         lax.fori_loop(0, 4, edges, 0)
         ghost_copy(unit).start()
@@ -396,6 +400,11 @@
         def _():
             setup()
 
+        @pl.when(v == units + 1)
+        def _():
+            for unit in range(units - 8, units):
+                ghost_copy(unit).wait_send()
+
         @pl.when((v >= 12) & (v % 4 == 0))
         def _():
             analysis(v // 4 - 3)
@@ -406,15 +415,9 @@
         return carry
     lax.fori_loop(0, units + 9, step, 0)
 
-    def finish(patch, carry):
-        @pl.when(patch >= patches - 2)
-        def _():
-            for dslot in range(3):
-                wait_sent(patch, dslot)
-        for dslot in range(4):
-            ghost_copy(patch * 4 + dslot).wait_send()
-        return carry
-    lax.fori_loop(0, patches, finish, 0)
+    for patch in range(patches - 2, patches):
+        for dslot in range(3):
+            wait_sent(patch, dslot)
 
 
 def update_kernel(done, tt_ref, g_ref, out_hbm, stage, sem):
@@ -477,7 +480,7 @@
                 pltpu.VMEM((7, 4, columns, members, 128), bf),
                 pltpu.VMEM((6, 50, members, 128), bf),
                 pltpu.VMEM((patches * 3, 50, members, 128), bf),
-                pltpu.VMEM((units, 2, 4, members, CP), bf),
+                pltpu.VMEM((8, 2, 4, members, CP), bf),
                 pltpu.VMEM((units, 2, 4, members, CP), bf),
                 pltpu.VMEM((2 * CP, 512), bf),
                 pltpu.VMEM((512, CP), bf),

time: 203 us -> 202 us (level)
  no operation moved by 1% of the time
where the time goes in v14:
time: 202 us
  Pallas kernels  202 us (100%)
    pallas_call x1, Pallas kernels, local_step(): pl.pallas_call(functools.partial(exchange_kernel, dims), out_shape=(pltpu...  196 us
    pallas_call x1, Pallas kernels, local_step(): pl.pallas_call(functools.partial(update_kernel, done), out_shape=jax.Shap...  6.12 us

profile of v14, /device:TPU:1, one launch (start us, length us, event | category | flops | bytes accessed | tf_op | source)
XLA Modules:
  0.0 202.0 jit_solution(13274762589724614287)
XLA Ops:
  0.0 195.9 %shard_map.64 = (bf16[8,4,16,64,256]{4,3,2,1,0:T(8,128)(2,1)S(1)}, f32[8,64,64]{2,1,0:T(8,128)S(1)}) custom-call(bf16[16,227,16,128]{3,2,1,0:T(8,128)(2,1)} %bitcast.3, bf16[454,512]{1,0:T(8,128)(2,1)} %wi_ref.1, bf16[227,512]{1,0:T(8,128)(2,1)} %bitcast.4, bf16[32,227]{1,0:T(8,128)(2,1)} %bitcast.5, f32[32,4,1,16,32]{4,3,2,1,0:T(8,128)} %yo_hbm.1, ...), custom_call_target="tpu_custom_call" | custom-call | tf_op jit(solution)/shard_map/pallas_call | solution.py:466
  195.9 6.1 %shard_map.65 = bf16[32,16,64,227]{3,2,1,0:T(8,128)(2,1)} custom-call(f32[8,64,64]{2,1,0:T(8,128)S(1)} %get-tuple-element.7.tt_ref, bf16[8,4,16,64,256]{4,3,2,1,0:T(8,128)(2,1)S(1)} %get-tuple-element.8.g_ref), custom_call_target="tpu_custom_call" | custom-call | tf_op jit(solution)/shard_map/pallas_call | solution.py:499

commit v15 on v14

--- a/solution.py
+++ b/solution.py
@@ -90,9 +90,11 @@
     def x_copy(m):
         return pltpu.make_async_copy(xt_hbm.at[m], xn.at[m % 2], xsem.at[m % 2])
 
-    def ghost_copy(unit):
+    def ghost_copy(unit, pair):
+        two = pl.ds(pair * 2, 2)
         return pltpu.make_async_remote_copy(
-            src_ref=gsend.at[unit % 8], dst_ref=grecv.at[unit], send_sem=gssem.at[unit], recv_sem=grsem.at[unit],
+            src_ref=gsend.at[unit % 8, :, two], dst_ref=grecv.at[unit, :, two],
+            send_sem=gssem.at[unit, pair], recv_sem=grsem.at[unit, pair],
             device_id={"dom": 1 - mydom}, device_id_type=MESH)
 
     def pair_copies(patch, dslot, pair):
@@ -224,15 +226,17 @@
 
         @pl.when(unit >= 8)
         def _():
-            ghost_copy(unit - 8).wait_send()
+            for pair in range(2):
+                ghost_copy(unit - 8, pair).wait_send()
 
         def edges(r, carry):
             for h in range(2):
                 gsend[unit % 8, 0, r, :, h * 128:h * 128 + 128] = xs[slot, h, r + 1, pl.ds(23, members, stride=33), :].astype(jnp.bfloat16)
                 gsend[unit % 8, 1, r, :, h * 128:h * 128 + 128] = xs[slot, h, r + 1, pl.ds(8, members, stride=33), :].astype(jnp.bfloat16)
             return carry
-        lax.fori_loop(0, 4, edges, 0)
-        ghost_copy(unit).start()
+        for pair in range(2):
+            lax.fori_loop(pair * 2, pair * 2 + 2, edges, 0)
+            ghost_copy(unit, pair).start()
 
     def forecast(unit):
         patch, dslot = unit // ens_size, unit % ens_size
@@ -242,7 +246,6 @@
         @pl.when((dslot < 3) & (patch >= 2))
         def _():
             wait_sent(patch - 2, dslot)
-        ghost_copy(unit).wait_recv()
 
         def block(r, carry):
             for h in range(2):
@@ -282,6 +285,7 @@
             sb2[out_slot, pair * 25 + 24] = left.astype(jnp.bfloat16)
 
         def half_unit(pair, carry):
+            ghost_copy(unit, pair).wait_recv()
             lax.fori_loop(pair * 2, pair * 2 + 2, block, 0)
 
             @pl.when(dslot < 3)
@@ -403,7 +407,8 @@
         @pl.when(v == units + 1)
         def _():
             for unit in range(units - 8, units):
-                ghost_copy(unit).wait_send()
+                for pair in range(2):
+                    ghost_copy(unit, pair).wait_send()
 
         @pl.when((v >= 12) & (v % 4 == 0))
         def _():
@@ -492,7 +497,7 @@
                 pltpu.VMEM((8, total_m, CP), f32),
                 pltpu.VMEM((2, total_m, 2 * total_m), f32),
                 pltpu.VMEM((2, total_m, 2 * total_m), f32),
-                dma((2,)), dma((units,)), dma((units,)), dma((patches, 3, 4)), dma((patches, 3, 4)), dma((2,)),
+                dma((2,)), dma((units, 2)), dma((units, 2)), dma((patches, 3, 4)), dma((patches, 3, 4)), dma((2,)),
             ],
             compiler_params=pltpu.CompilerParams(collective_id=0, has_side_effects=True, vmem_limit_bytes=46 * 1024 * 1024),
         )(ens_state.transpose(0, 3, 2, 1), w_in, w_out.T, obs_op.T, obs_val, obs_wt)

time: 202 us -> 203 us (level)
  no operation moved by 1% of the time
where the time goes in v15:
time: 203 us; the launch traced here: 202 us
  Pallas kernels  202 us (100%)
    pallas_call x1, Pallas kernels, local_step(): pl.pallas_call(functools.partial(exchange_kernel, dims), out_shape=(pltpu...  196 us
    pallas_call x1, Pallas kernels, local_step(): pl.pallas_call(functools.partial(update_kernel, done), out_shape=jax.Shap...  6.12 us

profile of v15, /device:TPU:1, one launch (start us, length us, event | category | flops | bytes accessed | tf_op | source)
XLA Modules:
  0.0 202.4 jit_solution(9760527916410947713)
XLA Ops:
  0.0 196.2 %shard_map.64 = (bf16[8,4,16,64,256]{4,3,2,1,0:T(8,128)(2,1)S(1)}, f32[8,64,64]{2,1,0:T(8,128)S(1)}) custom-call(bf16[16,227,16,128]{3,2,1,0:T(8,128)(2,1)} %bitcast.3, bf16[454,512]{1,0:T(8,128)(2,1)} %wi_ref.1, bf16[227,512]{1,0:T(8,128)(2,1)} %bitcast.4, bf16[32,227]{1,0:T(8,128)(2,1)} %bitcast.5, f32[32,4,1,16,32]{4,3,2,1,0:T(8,128)} %yo_hbm.1, ...), custom_call_target="tpu_custom_call" | custom-call | tf_op jit(solution)/shard_map/pallas_call | solution.py:471
  196.3 6.1 %shard_map.65 = bf16[32,16,64,227]{3,2,1,0:T(8,128)(2,1)} custom-call(f32[8,64,64]{2,1,0:T(8,128)S(1)} %get-tuple-element.7.tt_ref, bf16[8,4,16,64,256]{4,3,2,1,0:T(8,128)(2,1)S(1)} %get-tuple-element.8.g_ref), custom_call_target="tpu_custom_call" | custom-call | tf_op jit(solution)/shard_map/pallas_call | solution.py:504

commit v16 on v14

--- a/solution.py
+++ b/solution.py
@@ -166,10 +166,10 @@
                 x_copy(m + 1).wait()
             for col in range(columns):
                 turn_column(odd, col)
-                for c in range(channels * col // columns, channels * (col + 1) // columns):
-                    widen(1 - odd, c)
                 for row in range(rows * col // columns, rows * (col + 1) // columns):
                     narrow(1 - odd, jnp.maximum(m - 1, 0), row)
+            for c in range(channels):
+                widen(1 - odd, c)
         return carry
     for ref in (wide[0][1][3], wide[1][1][3]):
         ref[17 * (channels % 32):544, :] = jnp.zeros((544 - 17 * (channels % 32), 128), jnp.float32)

time: 202 us -> 202 us (level)
  no operation moved by 1% of the time
where the time goes in v16:
time: 202 us
  Pallas kernels  202 us (100%)
    pallas_call x1, Pallas kernels, local_step(): pl.pallas_call(functools.partial(exchange_kernel, dims), out_shape=(pltpu...  196 us
    pallas_call x1, Pallas kernels, local_step(): pl.pallas_call(functools.partial(update_kernel, done), out_shape=jax.Shap...  6.12 us

profile of v16, /device:TPU:1, one launch (start us, length us, event | category | flops | bytes accessed | tf_op | source)
XLA Modules:
  0.0 202.0 jit_solution(18360910369795104102)
XLA Ops:
  0.0 195.9 %shard_map.64 = (bf16[8,4,16,64,256]{4,3,2,1,0:T(8,128)(2,1)S(1)}, f32[8,64,64]{2,1,0:T(8,128)S(1)}) custom-call(bf16[16,227,16,128]{3,2,1,0:T(8,128)(2,1)} %bitcast.3, bf16[454,512]{1,0:T(8,128)(2,1)} %wi_ref.1, bf16[227,512]{1,0:T(8,128)(2,1)} %bitcast.4, bf16[32,227]{1,0:T(8,128)(2,1)} %bitcast.5, f32[32,4,1,16,32]{4,3,2,1,0:T(8,128)} %yo_hbm.1, ...), custom_call_target="tpu_custom_call" | custom-call | tf_op jit(solution)/shard_map/pallas_call | solution.py:466
  195.9 6.1 %shard_map.65 = bf16[32,16,64,227]{3,2,1,0:T(8,128)(2,1)} custom-call(f32[8,64,64]{2,1,0:T(8,128)S(1)} %get-tuple-element.7.tt_ref, bf16[8,4,16,64,256]{4,3,2,1,0:T(8,128)(2,1)S(1)} %get-tuple-element.8.g_ref), custom_call_target="tpu_custom_call" | custom-call | tf_op jit(solution)/shard_map/pallas_call | solution.py:499
